TPU v7x, 32 devices: a whole 2x2x4 slice. The times are simulated.
32 devices in a mesh: stream: 8 (over z, x), span: 4 (over y, core).
Axes of the slice: x: 2, y: 2, z: 4, core: 2. Of those that a mesh axis runs over, the one named last changes fastest.
Arguments:
- state: float32 [320, 8, 625], P('stream', 'span'), may hold values from -0.25 to 2.5, as said below
- direction: float32 [320, 8, 625], P('stream', 'span'), may hold values from -6 to 6
- metric: float32 [320, 8, 3], P('stream', 'span'), may hold values from 1 to 4
- face_source: int32 [320, 4], P('stream'), may hold values from -1 to 225, as said below
- send_rows: int32 [8, 2, 33], P('stream'), may hold values from 0 to 159, as said below
Outputs:
- residual: float32 [320, 8, 625], P('stream', 'span')
- basis_next: float32 [320, 8, 625], P('stream', 'span')
- krylov: float32 [3], replicated
Inputs may be any that keep to these rules, and one draw needn't show every extreme that they name: `state`: conserved variables from density 0.75 to 1.25, flow-wise velocity 0.1 to 0.5, other velocities -0.2 to 0.2, pressure 0.5 to 0.9, so pressure and temperature are positive. `face_source`: the plane is a grid of columns of 32 cells, numbered column by column, partition d owning cells d * 40 to (d + 1) * 40 - 1 in a random local order; flow-wise faces wrap around. Every face neighbour lies in the same or an adjacent partition; -1 stands exactly on the lower face of the lowest and the upper face of the highest row; indices into received blocks point at used slots. `send_rows`: at most 33 faces per neighbouring pair, and some pair uses all 33; slots beyond a pair's count hold 0; the order of slots is the order in which the receiver's face_source refers to them.
All inputs are finite; a program needn't handle non-finite values.
Results may differ from a plain program's by a relative error of at most 0.0003.
Values sent between devices are 32-bit elements.
A program may use at most 128 MiB of HBM per device.

v0:
```python
import functools
import math

import jax
import jax.numpy as jnp
import numpy as np
from jax import lax
from jax.experimental import pallas as pl
from jax.experimental.pallas import tpu as pltpu
from jax.sharding import PartitionSpec as P

GAMMA = 1.4
VISC = 0.01
COND = VISC * GAMMA / ((GAMMA - 1.0) * 0.72)
LIFT = 10.0
MESH = pl.DeviceIdType.MESH
F32, BF16 = jnp.float32, jnp.bfloat16


def diff_table():
    spread = math.sqrt(3.0 / 7.0)
    points = np.array([-1.0, -spread, 0.0, spread, 1.0])
    weights = np.array(
        [np.prod([points[i] - points[j] for j in range(5) if j != i]) for i in range(5)]
    )
    matrix = np.zeros((5, 5))
    for i in range(5):
        for j in range(5):
            if i != j:
                matrix[i, j] = weights[i] / (weights[j] * (points[i] - points[j]))
        matrix[i, i] = np.sum([1.0 / (points[i] - points[j]) for j in range(5) if j != i])
    return matrix


def operators(layers):
    table = diff_table()
    eye = np.eye(5)
    kron = [
        np.einsum("ai,bj,ck->ijkabc", *[table if m == a else eye for m in range(3)]).reshape(125, 125)
        for a in range(3)
    ]
    node = np.arange(125).reshape(5, 5, 5)
    vw, fw, half = 128 * layers, 64 * layers, 32 * layers
    deriv = np.zeros((3, vw, vw), np.float32)
    pick = np.zeros((3, vw, fw), np.float32)
    for a in range(3):
        for l in range(layers):
            b = 128 * l
            deriv[a, b : b + 125, b : b + 125] = kron[a]
            for side in range(2):
                face = np.take(node, 4 * side, axis=a).reshape(-1)
                for m, at in enumerate(face):
                    pick[a, b + at, side * half + 32 * l + m] = 1.0
    high = deriv.astype(jnp.bfloat16)
    low = (deriv - high.astype(np.float32)).astype(jnp.bfloat16)
    lift = np.swapaxes(pick, 1, 2)
    return high, low, pick.astype(jnp.bfloat16), lift.astype(jnp.bfloat16)


def pieces(x, n):
    out = []
    for i in range(n):
        p = x.astype(BF16)
        out.append(p)
        if i + 1 < n:
            x = x - p.astype(F32)
    return out


def dot(a, b):
    return jnp.dot(a, b, preferred_element_type=F32)


def left(x, w, n):
    return sum(dot(p, w) for p in pieces(x, n)[::-1])


def right(w, x, n):
    return sum(dot(w, p) for p in pieces(x, n)[::-1])


def derive(x, high, low):
    a, b = pieces(x, 2)
    return dot(a, low) + dot(b, high) + dot(a, high)


def fields_of(u):
    inv = 1.0 / u[0]
    vel = [u[1] * inv, u[2] * inv, u[3] * inv]
    kinetic = 0.5 * (u[1] * vel[0] + u[2] * vel[1] + u[3] * vel[2])
    pressure = (GAMMA - 1.0) * (u[4] - kinetic)
    return vel, pressure, pressure * inv


def inviscid(u, a):
    vel, pressure, _ = fields_of(u)
    out = [u[1 + a]]
    for m in range(3):
        term = u[1 + m] * vel[a]
        out.append(term + pressure if m == a else term)
    out.append((u[4] + pressure) * vel[a])
    return out


def viscous(vel, q, a, divergence):
    stress = []
    for m in range(3):
        term = q[a][m] + q[m][a]
        if m == a:
            term = term - 2.0 / 3.0 * divergence
        stress.append(VISC * term)
    energy = stress[0] * vel[0] + stress[1] * vel[1] + stress[2] * vel[2] + COND * q[a][3]
    return stress + [energy]


def viscous_all(u, q):
    inv = 1.0 / u[0]
    vel = [u[1] * inv, u[2] * inv, u[3] * inv]
    divergence = q[0][0] + q[1][1] + q[2][2]
    return [viscous(vel, q, a, divergence) for a in range(3)]


def gradient_fields(u):
    vel, _, temper = fields_of(u)
    return vel + [temper]


def jump_fields(inner, outer):
    return [o - i for o, i in zip(gradient_fields(outer), gradient_fields(inner))]


def surface(inner, outer, sign, a):
    vi, pi, ti = fields_of(inner)
    vo, po, to = fields_of(outer)
    square = sum(v * v for v in vi) + GAMMA * ti + sum(v * v for v in vo) + GAMMA * to
    speed = jnp.sqrt(0.5 * square)
    fi, fo = inviscid(inner, a), inviscid(outer, a)
    return [
        (0.5 * LIFT) * (sign * (fo[m] - fi[m]) - speed * (outer[m] - inner[m])) for m in range(5)
    ]


def ratio(top, bottom):
    return jnp.where(bottom > 0.0, top / jnp.where(bottom > 0.0, bottom, 1.0), 0.0)


def kernel(
    ns, np_,
    x_hbm, d_hbm, metric_hbm, fs_hbm, sr_hbm, key_hbm, dh_hbm, dl_hbm, pick_hbm, lift_hbm,
    res_hbm, prod_hbm, table_ref,
    u, uf, of, w, jf, q, v, vf, ov, g, s, r, mv, mf,
    sb1, rb1, zs1, zr1, sb2, rb2, zs2, zr2, st, sta,
    x_ref, d_ref, metric_ref, fs_ref, sr_ref, keyrow_ref, dh_ref, dl_ref, pick_ref, lift_ref,
    xsend, xrecv, asend, arecv, loads, store, res, prod,
):
    C, L = x_ref.shape[0], x_ref.shape[1]
    VW, FW, half = 128 * L, 64 * L, 32 * L
    SLOTS = sr_ref.shape[2]
    SP = -(-SLOTS // 8) * 8
    MAIN, REM = SLOTS // 8, SLOTS % 8
    OWN = 4 * C
    ms, mp = lax.axis_index("stream"), lax.axis_index("span")
    lower, upper = lax.rem(ms + ns - 1, ns), lax.rem(ms + 1, ns)
    below, above = lax.rem(mp + np_ - 1, np_), lax.rem(mp + 1, np_)

    inputs = [
        pltpu.make_async_copy(src, dst, loads.at[i])
        for i, (src, dst) in enumerate(
            [
                (x_hbm, x_ref), (d_hbm, d_ref), (pick_hbm, pick_ref), (key_hbm, keyrow_ref),
                (fs_hbm, fs_ref), (sr_hbm, sr_ref), (metric_hbm, metric_ref),
                (dh_hbm, dh_ref), (dl_hbm, dl_ref), (lift_hbm, lift_ref),
            ]
        )
    ]
    for copy in inputs:
        copy.start()

    def peer(k):
        a, b = divmod(k, np_)
        return lax.rem(ms + a, ns), lax.rem(mp + b, np_)

    everyone = ns * np_
    barrier = pltpu.get_barrier_semaphore()
    for k in range(1, everyone):
        pl.semaphore_signal(barrier, inc=1, device_id=peer(k), device_id_type=MESH)

    fl = lax.broadcasted_iota(jnp.int32, (1, FW), 1)
    vl = lax.broadcasted_iota(jnp.int32, (1, VW), 1)
    first = fl < half
    sign = jnp.where(first, -1.0, 1.0)
    flayer = lax.rem(fl, half) // 32
    fnode = lax.rem(fl, 32)
    fpad = jnp.where(fnode >= 25, 1.0, 0.0)

    def roll(x, shift):
        shift = shift % FW
        return pltpu.roll(x, shift, 1) if shift else x

    di = lax.broadcasted_iota(jnp.int32, (C, C), 0)
    dj = lax.broadcasted_iota(jnp.int32, (C, C), 1)

    def column(row):
        return jnp.sum(jnp.where(di == dj, row, 0.0), axis=1, keepdims=True)

    for copy in inputs[:2]:
        copy.wait()

    for pt, ref in enumerate((x_ref, d_ref)):
        for l in range(L):
            for m in range(5):
                pad = 1.0 if pt == 0 and m % 4 == 0 else 0.0
                u[pt, m, :, 128 * l + 120 : 128 * (l + 1)] = jnp.full((C, 8), pad, F32)
                u[pt, m, :, 128 * l : 128 * l + 125] = ref[:, l, 125 * m : 125 * (m + 1)]
    for copy in inputs[2:7]:
        copy.wait()
    keyrow = keyrow_ref[...].astype(F32)
    source = [column(fs_ref[f : f + 1, :].astype(F32)) for f in range(4)]
    onehot = jnp.concatenate(
        [
            jnp.where(source[2 * a + side] == keyrow, 1.0, 0.0)
            for side in range(2)
            for a in range(2)
        ],
        axis=0,
    ).astype(BF16)
    hot_own, hot_recv = onehot[:, :OWN], onehot[:, OWN : OWN + 2 * SP]
    ri = lax.broadcasted_iota(jnp.int32, (SP, SLOTS), 0)
    li = lax.broadcasted_iota(jnp.int32, (SP, SLOTS), 1)
    send_hot = []
    for side in range(2):
        row = sr_ref[0, side : side + 1, :].astype(F32)
        wanted = jnp.sum(jnp.where(ri == li, row, 0.0), axis=1, keepdims=True)
        send_hot.append(jnp.where(wanted == keyrow[:, :OWN], 1.0, 0.0))
    send_hot = jnp.concatenate(send_hot, axis=0).astype(BF16)

    def swap(a, b):
        return (
            jnp.where(first, a, pltpu.roll(b, half, 1)),
            jnp.where(first, pltpu.roll(a, half, 1), b),
        )

    def exchange(faces, members, sb, rb, zs, zr, base):
        blocks = [[swap(faces(0, m, a), faces(1, m, a)) for m in range(members)] for a in range(3)]
        table = jnp.concatenate(
            [
                jnp.concatenate([blocks[a][m][side] for m in range(members)], axis=1)
                for side in range(2)
                for a in range(2)
            ],
            axis=0,
        )
        for m in range(0, members, 2):
            for side in range(2):
                value = blocks[2][m][side]
                if m + 1 < members:
                    other = roll(blocks[2][m + 1][side], 32 if side == 0 else -32)
                    value = jnp.where(flayer == (0 if side == 0 else L - 1), value, other)
                zs[side, :, FW * (m // 2) : FW * (m // 2 + 1)] = value
        zs_copies = [
            (zs.at[0], zr.at[1], (ms, below)),
            (zs.at[1], zr.at[0], (ms, above)),
        ]
        copies = []
        for i, (src, dst, to) in enumerate(zs_copies):
            copies.append(
                pltpu.make_async_remote_copy(
                    src_ref=src, dst_ref=dst, send_sem=xsend.at[base + i],
                    recv_sem=xrecv.at[base + i], device_id=to, device_id_type=MESH,
                )
            )
        table_pieces = pieces(table, 3)
        sent = sum(dot(send_hot, p) for p in table_pieces[::-1])
        return blocks, table_pieces, sent, copies

    def finish_send(sent, sb, rb, base):
        for m in range(4):
            value = sent[:, FW * m : FW * (m + 1)]
            if sent.shape[1] > 4 * FW:
                spare = roll(sent[:, 4 * FW :], 25 - 7 * m)
                value = jnp.where(fnode < 25, value, spare)
            for side in range(2):
                for b in range(MAIN):
                    at = side * SP + 8 * b
                    sb[side, 4 * b + m] = value[at : at + 8]
                for e in range(REM):
                    at, to = side * SP + 8 * MAIN + e, REM * m + e
                    sb[side, 4 * MAIN + to // 8, to % 8 : to % 8 + 1, :] = value[at : at + 1]
        out = []
        for i, (src, dst, to) in enumerate(
            [
                (sb.at[0], rb.at[1], (lower, mp)),
                (sb.at[1], rb.at[0], (upper, mp)),
            ]
        ):
            out.append(
                pltpu.make_async_remote_copy(
                    src_ref=src, dst_ref=dst, send_sem=xsend.at[base + 2 + i],
                    recv_sem=xrecv.at[base + 2 + i], device_id=to, device_id_type=MESH,
                )
            )
        return out

    def plane_outside(own, rb, members, put):
        row8 = lax.broadcasted_iota(jnp.int32, (8, 1), 0)
        rows = []
        for side in range(2):
            rows += [
                jnp.concatenate([rb[side, 4 * b + m] for m in range(4)], axis=1)
                for b in range(MAIN)
            ]
            if REM:
                parts = []
                for m in range(4):
                    part = jnp.zeros((8, FW), F32)
                    for e in range(REM):
                        to = REM * m + e
                        line = rb[side, 4 * MAIN + to // 8, to % 8 : to % 8 + 1, :]
                        part = jnp.where(row8 == e, line, part)
                    parts.append(part)
                rows.append(jnp.concatenate(parts, axis=1))
        received = jnp.concatenate(rows, axis=0)
        if members * FW > received.shape[1]:
            spare = jnp.zeros((2 * SP, FW), F32)
            for m in range(received.shape[1] // FW):
                part = roll(received[:, FW * m : FW * (m + 1)], 7 * m - 25)
                spare = jnp.where((fnode >= 7 * m) & (fnode < 7 * m + 7), part, spare)
            received = jnp.concatenate([received, spare], axis=1)
        got = own + right(hot_recv, received, 3)
        for a in range(2):
            for m in range(members):
                lanes = slice(FW * m, FW * (m + 1))
                lo = got[a * C : (a + 1) * C, lanes]
                hi = got[(2 + a) * C : (3 + a) * C, lanes]
                primal, tangent = swap(lo, hi)
                put(0, m, a, primal)
                put(1, m, a, tangent)

    def layer_outside(blocks, zr, members, put):
        for m in range(members):
            lanes = slice(FW * (m // 2), FW * (m // 2 + 1))
            step = 32 * (L - 1 if m % 2 == 0 else L - 2)
            lo = jnp.where(flayer == 0, roll(zr[0, :, lanes], -step), roll(blocks[2][m][1], 32))
            hi = jnp.where(flayer == L - 1, roll(zr[1, :, lanes], step), roll(blocks[2][m][0], -32))
            primal, tangent = swap(lo, hi)
            put(0, m, 2, primal)
            put(1, m, 2, tangent)

    whole = u[...].reshape(10 * C, VW)
    for a in range(3):
        faces = left(whole, pick_ref[a], 3).reshape(2, 5, C, FW)
        for m in range(5):
            uf[0, m, a] = faces[0, m] + fpad if m % 4 == 0 else faces[0, m]
            uf[1, m, a] = faces[1, m]
    blocks1, table1, sent1, zcopies1 = exchange(
        lambda pt, m, a: uf[pt, m, a], 5, sb1, rb1, zs1, zr1, 0
    )
    pcopies1 = finish_send(sent1, sb1, rb1, 0)
    pl.semaphore_wait(barrier, everyone - 1)
    for copy in pcopies1 + zcopies1:
        copy.start()
    for a in range(3):
        wide = jnp.zeros((C, VW), F32)
        face = jnp.zeros((C, FW), F32)
        for l in range(L):
            value = column(metric_ref[a, l : l + 1, :])
            wide = jnp.where(vl // 128 == l, value, wide)
            face = jnp.where(flayer == l, value, face)
        mv[a] = wide
        mf[a] = face

    for copy in inputs[7:]:
        copy.wait()

    own1 = sum(dot(hot_own, p) for p in table1[::-1])

    @pl.loop(0, C // 8, unroll=True)
    def _(i):
        rows = pl.ds(pl.multiple_of(i * 8, 8), 8)
        primal = [u[0, m, rows, :] for m in range(5)]
        tangent = [u[1, m, rows, :] for m in range(5)]
        fp, ft = jax.jvp(gradient_fields, (primal,), (tangent,))
        for m in range(4):
            w[0, m, rows, :] = fp[m]
            w[1, m, rows, :] = ft[m]

    fields = w[...].reshape(8 * C, VW)
    for a in range(3):
        q[a] = derive(fields, dh_ref[a], dl_ref[a]).reshape(2, 4, C, VW)

    for copy in zcopies1 + pcopies1:
        copy.wait()
    low_wall = jnp.where(source[2] < 0.0, 1.0, 0.0)
    high_wall = jnp.where(source[3] < 0.0, 1.0, 0.0)
    wall = jnp.where(first, low_wall, high_wall) > 0.5

    def put1(pt, m, a, value):
        if a == 1:
            own = uf[pt, m, a]
            value = jnp.where(wall, own if m % 4 == 0 else -own, value)
        of[pt, m, a] = jnp.where(fnode < 25, value, uf[pt, m, a])

    plane_outside(own1, rb1, 5, put1)
    layer_outside(blocks1, zr1, 5, put1)

    for a in range(3):
        @pl.loop(0, C // 8, unroll=True)
        def _(i):
            rows = pl.ds(pl.multiple_of(i * 8, 8), 8)
            primal = ([uf[0, m, a, rows, :] for m in range(5)], [of[0, m, a, rows, :] for m in range(5)])
            tangent = ([uf[1, m, a, rows, :] for m in range(5)], [of[1, m, a, rows, :] for m in range(5)])
            jp, jt = jax.jvp(jump_fields, primal, tangent)
            for m in range(4):
                jf[a, 0, m, rows, :] = (0.5 * LIFT) * sign * jp[m]
                jf[a, 1, m, rows, :] = (0.5 * LIFT) * sign * jt[m]

        q[a] += left(jf[a].reshape(8 * C, FW), lift_ref[a], 2).reshape(2, 4, C, VW)

    @pl.loop(0, C // 8, unroll=True)
    def _(i):
        rows = pl.ds(pl.multiple_of(i * 8, 8), 8)
        scale = [mv[a, rows, :] for a in range(3)]
        states = [[u[pt, m, rows, :] for m in range(5)] for pt in range(2)]
        grads = [
            [[scale[a] * q[a, pt, m, rows, :] for m in range(4)] for a in range(3)]
            for pt in range(2)
        ]
        vp, vt = jax.jvp(viscous_all, (states[0], grads[0]), (states[1], grads[1]))
        for a in range(3):
            for m in range(4):
                v[a, 0, m, rows, :] = vp[a][m]
                v[a, 1, m, rows, :] = vt[a][m]

    for a in range(3):
        vf[a] = left(v[a].reshape(8 * C, VW), pick_ref[a], 3).reshape(2, 4, C, FW)
    blocks2, table2, sent2, zcopies2 = exchange(
        lambda pt, m, a: vf[a, pt, m], 4, sb2, rb2, zs2, zr2, 4
    )
    pcopies2 = finish_send(sent2, sb2, rb2, 4)
    for copy in pcopies2 + zcopies2:
        copy.start()

    own2 = sum(dot(hot_own, p) for p in table2[::-1])

    @pl.loop(0, C // 8, unroll=True)
    def _(i):
        rows = pl.ds(pl.multiple_of(i * 8, 8), 8)
        states = [[u[pt, m, rows, :] for m in range(5)] for pt in range(2)]
        for a in range(3):
            scale = mv[a, rows, :]
            fluxes = jax.jvp(lambda x: inviscid(x, a), (states[0],), (states[1],))
            for pt in range(2):
                g[a, pt, 0, rows, :] = scale * fluxes[pt][0]
                for m in range(4):
                    g[a, pt, m + 1, rows, :] = scale * (fluxes[pt][m + 1] - v[a, pt, m, rows, :])

    for a in range(3):
        @pl.loop(0, C // 8, unroll=True)
        def _(i):
            rows = pl.ds(pl.multiple_of(i * 8, 8), 8)
            primal = ([uf[0, m, a, rows, :] for m in range(5)], [of[0, m, a, rows, :] for m in range(5)])
            tangent = ([uf[1, m, a, rows, :] for m in range(5)], [of[1, m, a, rows, :] for m in range(5)])
            sp, stt = jax.jvp(
                lambda inner, outer: surface(inner, outer, sign, a), primal, tangent
            )
            for m in range(5):
                s[a, 0, m, rows, :] = sp[m]
                s[a, 1, m, rows, :] = stt[m]

    total = None
    for a in range(3):
        part = derive(g[a].reshape(10 * C, VW), dh_ref[a], dl_ref[a])
        total = part if total is None else total + part
    r[...] = total.reshape(2, 5, C, VW)

    for copy in zcopies2 + pcopies2:
        copy.wait()

    def put2(pt, m, a, value):
        if a == 1:
            value = jnp.where(wall, vf[a, pt, m], value)
        ov[a, pt, m] = value

    plane_outside(own2, rb2, 4, put2)
    layer_outside(blocks2, zr2, 4, put2)
    lifted = None
    for a in range(3):
        for pt in range(2):
            s[a, pt, 0] = mf[a] * s[a, pt, 0]
            for m in range(4):
                jump = ov[a, pt, m] - vf[a, pt, m]
                s[a, pt, m + 1] = mf[a] * (s[a, pt, m + 1] - (0.5 * LIFT) * sign * jump)
        part = left(s[a].reshape(10 * C, FW), lift_ref[a], 2)
        lifted = part if lifted is None else lifted + part
    r[...] += lifted.reshape(2, 5, C, VW)

    def whole_sum(parts):
        acc = parts[0]
        for part in parts[1:]:
            acc = acc + part
        return jnp.sum(jnp.sum(acc, axis=0, keepdims=True), axis=1, keepdims=True)

    pd = whole_sum([r[1, m] * u[1, m] for m in range(5)])
    dd = whole_sum([u[1, m] * u[1, m] for m in range(5)])
    rs = whole_sum([r[0, m] * r[0, m] for m in range(5)])
    mine = ratio(pd, dd)
    rests = [r[1, m] - mine * u[1, m] for m in range(5)]
    rr = whole_sum([x * x for x in rests])
    rd = whole_sum([x * u[1, m] for m, x in enumerate(rests)])
    lane = lax.broadcasted_iota(jnp.int32, (1, 128), 1)
    row = jnp.zeros((1, 128), F32)
    for i, value in enumerate((pd, dd, rs, rr, rd)):
        row = jnp.where(lane == i, value, row)
    st[...] = row
    copies = [
        pltpu.make_async_remote_copy(
            src_ref=st, dst_ref=sta.at[k], send_sem=asend.at[k], recv_sem=arecv.at[k],
            device_id=peer(k), device_id_type=MESH,
        )
        for k in range(1, everyone)
    ]
    for copy in copies:
        copy.start()
    sta[0] = st[...]
    writes = []
    for pt, (part, out) in enumerate([(res, res_hbm), (prod, prod_hbm)]):
        for l in range(L):
            for m in range(5):
                part[:, l, 125 * m : 125 * (m + 1)] = r[pt, m, :, 128 * l : 128 * l + 125]
        writes.append(pltpu.make_async_copy(part, out, store.at[pt]))
        writes[pt].start()
    for copy in copies:
        copy.wait()
    table_ref[...] = sta[...].reshape(everyone, 128)
    for copy in writes:
        copy.wait()


def finish(
    total_count, part_hbm, prod_hbm, d_hbm, table_hbm, res_hbm, basis_hbm, kry_ref,
    res, prod, d, table_ref, basis, sems,
):
    loads = [
        pltpu.make_async_copy(src, dst, sems.at[i])
        for i, (src, dst) in enumerate(
            [(part_hbm, res), (table_hbm, table_ref), (d_hbm, d), (prod_hbm, prod)]
        )
    ]
    for copy in loads:
        copy.start()
    loads[0].wait()
    first = pltpu.make_async_copy(res, res_hbm, sems.at[4])
    first.start()
    for copy in loads[1:]:
        copy.wait()
    lane = lax.broadcasted_iota(jnp.int32, (1, 128), 1)
    table = table_ref[...]
    pd, dd, rs, rr, rd = [
        jnp.sum(jnp.where(lane == i, table, 0.0), axis=1, keepdims=True) for i in range(5)
    ]
    coefficient = jnp.sum(pd, axis=0, keepdims=True) * (1.0 / total_count)
    shift = ratio(pd, dd) - coefficient
    rr = jnp.sum(rr + 2.0 * shift * rd + shift * shift * dd, axis=0, keepdims=True)
    rs = jnp.sum(rs, axis=0, keepdims=True)
    beta = jnp.sqrt(rr * (1.0 / total_count))
    norm = jnp.sqrt(rs * (1.0 / total_count))
    row = jnp.where(lane == 0, coefficient, jnp.where(lane == 1, beta, norm))
    kry_ref[...] = row[0, :3]
    c, inv = coefficient, 1.0 / beta
    basis[...] = (prod[...] - c[:, :, None] * d[...]) * inv[:, :, None]
    second = pltpu.make_async_copy(basis, basis_hbm, sems.at[5])
    second.start()
    first.wait()
    second.wait()


def local(ns, np_, state, direction, metric, face_source, send_rows):
    C, L, width = state.shape
    slots = send_rows.shape[2]
    SP = -(-slots // 8) * 8
    VW, FW = 128 * L, 64 * L
    own = 4 * C
    keys = np.full((1, own + 2 * SP), -7, np.int32)
    side, rest = np.divmod(np.arange(own), 2 * C)
    keys[0, :own] = 4 * (rest % C) + 2 * (rest // C) + side
    keys[0, own : own + slots] = own + np.arange(slots)
    keys[0, own + SP : own + SP + slots] = own + slots + np.arange(slots)
    tiles = 4 * (slots // 8) + -(-4 * (slots % 8) // 8)
    high, low, pick, lift = operators(L)
    operands = (
        state, direction, jnp.transpose(metric, (2, 1, 0)), face_source.T, send_rows,
        *[jnp.asarray(x) for x in (keys, high, low, pick, lift)],
    )
    vmem = lambda *shape: pltpu.VMEM(shape, F32)
    dma = lambda n: pltpu.SemaphoreType.DMA((n,))
    spec = pl.BlockSpec(memory_space=pltpu.VMEM)
    parts, product, table = pl.pallas_call(
        functools.partial(kernel, ns, np_),
        out_shape=(
            jax.ShapeDtypeStruct(state.shape, F32),
            jax.ShapeDtypeStruct(state.shape, F32),
            jax.ShapeDtypeStruct((ns * np_, 128), F32),
        ),
        in_specs=[pl.BlockSpec(memory_space=pltpu.HBM)] * 10,
        out_specs=(pl.BlockSpec(memory_space=pltpu.HBM),) * 2 + (spec,),
        scratch_shapes=[
            vmem(2, 5, C, VW), vmem(2, 5, 3, C, FW), vmem(2, 5, 3, C, FW),
            vmem(2, 4, C, VW), vmem(3, 2, 4, C, FW), vmem(3, 2, 4, C, VW),
            vmem(3, 2, 4, C, VW), vmem(3, 2, 4, C, FW), vmem(3, 2, 4, C, FW),
            vmem(3, 2, 5, C, VW), vmem(3, 2, 5, C, FW), vmem(2, 5, C, VW),
            vmem(3, C, VW), vmem(3, C, FW),
            vmem(2, tiles, 8, FW), vmem(2, tiles, 8, FW), vmem(2, C, 3 * FW), vmem(2, C, 3 * FW),
            vmem(2, tiles, 8, FW), vmem(2, tiles, 8, FW), vmem(2, C, 2 * FW), vmem(2, C, 2 * FW),
            vmem(1, 128), vmem(ns * np_, 1, 128),
            *[pltpu.VMEM(x.shape, x.dtype) for x in operands],
            dma(8), dma(8), dma(ns * np_), dma(ns * np_), dma(10), dma(2), vmem(C, L, width), vmem(C, L, width),
        ],
        compiler_params=pltpu.CompilerParams(
            collective_id=0, has_side_effects=True, vmem_limit_bytes=63 * 1024 * 1024
        ),
        name="navier",
    )(*operands)
    hbm = pl.BlockSpec(memory_space=pltpu.HBM)
    return pl.pallas_call(
        functools.partial(finish, float(state.size * ns * np_)),
        out_shape=(
            jax.ShapeDtypeStruct(state.shape, F32),
            jax.ShapeDtypeStruct(state.shape, F32),
            jax.ShapeDtypeStruct((3,), F32),
        ),
        in_specs=[hbm] * 4,
        out_specs=(hbm, hbm, spec),
        scratch_shapes=[
            vmem(C, L, width), vmem(C, L, width), vmem(C, L, width), vmem(ns * np_, 128),
            vmem(C, L, width), dma(6),
        ],
        compiler_params=pltpu.CompilerParams(vmem_limit_bytes=63 * 1024 * 1024),
        name="finish",
    )(parts, product, direction, table)


def solution(mesh):
    return jax.shard_map(
        functools.partial(local, mesh.shape["stream"], mesh.shape["span"]),
        mesh=mesh,
        in_specs=(
            P("stream", "span", None),
            P("stream", "span", None),
            P("stream", "span", None),
            P("stream", None),
            P("stream", None, None),
        ),
        out_specs=(P("stream", "span", None), P("stream", "span", None), P()),
        check_vma=False,
    )
```

profile of v0, /device:TPU:0, one launch (start us, length us, event | category | flops | bytes accessed | tf_op | source)
XLA Modules:
  0.0 29.6 jit_solution(8627987812115112573)
XLA Ops:
  0.6 26.5 %navier.1 = (f32[40,2,625]{2,1,0:T(2,128)}, f32[40,2,625]{2,1,0:T(2,128)}, f32[32,128]{1,0:T(8,128)}) custom-call(f32[40,2,625]{2,1,0:T(2,128)} %x_hbm.1, f32[40,2,625]{2,1,0:T(2,128)} %d_hbm.3, f32[3,2,40]{2,1,0:T(2,128)} %bitcast.2, s32[4,40]{1,0:T(4,128)} %bitcast.3, s32[1,2,33]{2,1,0:T(2,128)} %sr_hbm.1, s32[1,240]{1,0:T(1,128)} %constant.10.clone.key_hbm, ...), custom_call_target="tpu_custom_call" | custom-call | tf_op jit(solution)/shard_map/navier/pallas_call | solution.py:597
  27.1 2.5 %finish.1 = (f32[40,2,625]{2,1,0:T(2,128)}, f32[40,2,625]{2,1,0:T(2,128)}, f32[3]{0:T(128)}) custom-call(f32[40,2,625]{2,1,0:T(2,128)} %get-tuple-element.6.part_hbm, f32[40,2,625]{2,1,0:T(2,128)} %get-tuple-element.7.prod_hbm, f32[40,2,625]{2,1,0:T(2,128)} %d_hbm.3, f32[32,128]{1,0:T(8,128)} %get-tuple-element.8.table_hbm), custom_call_target="tpu_custom_call" | custom-call | tf_op jit(solution)/shard_map/finish/pallas_call | solution.py:624
where the time goes:
time: 29.8 us; the launch traced here: 29.6 us
  Pallas kernels  29 us (97%)
  between operations  0.64 us (2%)
    pallas_call x1, Pallas kernels, local(): pl.pallas_call(functools.partial(kernel, ns, np_), out_shape=(jax.ShapeDt...  26.5 us
    pallas_call x1, Pallas kernels, local(): pl.pallas_call(functools.partial(finish, float(state.size * ns * np_)), o...  2.54 us

commit v1 on v0

--- a/solution.py
+++ b/solution.py
@@ -54,7 +54,7 @@
     high = deriv.astype(jnp.bfloat16)
     low = (deriv - high.astype(np.float32)).astype(jnp.bfloat16)
     lift = np.swapaxes(pick, 1, 2)
-    return high, low, pick.astype(jnp.bfloat16), lift.astype(jnp.bfloat16)
+    return high, low, lift.astype(jnp.bfloat16)
 
 
 def pieces(x, n):
@@ -146,12 +146,12 @@
 
 def kernel(
     ns, np_,
-    x_hbm, d_hbm, metric_hbm, fs_hbm, sr_hbm, key_hbm, dh_hbm, dl_hbm, pick_hbm, lift_hbm,
-    res_hbm, prod_hbm, table_ref,
+    x_hbm, d_hbm, metric_hbm, fs_hbm, sr_hbm, key_hbm, dh_hbm, dl_hbm, lift_hbm,
+    res_ref, prod_ref, own_ref, table_ref,
     u, uf, of, w, jf, q, v, vf, ov, g, s, r, mv, mf,
     sb1, rb1, zs1, zr1, sb2, rb2, zs2, zr2, st, sta,
-    x_ref, d_ref, metric_ref, fs_ref, sr_ref, keyrow_ref, dh_ref, dl_ref, pick_ref, lift_ref,
-    xsend, xrecv, asend, arecv, loads, store, res, prod,
+    x_ref, d_ref, metric_ref, fs_ref, sr_ref, keyrow_ref, dh_ref, dl_ref, lift_ref,
+    xsend, xrecv, asend, arecv, loads,
 ):
     C, L = x_ref.shape[0], x_ref.shape[1]
     VW, FW, half = 128 * L, 64 * L, 32 * L
@@ -167,7 +167,7 @@
         pltpu.make_async_copy(src, dst, loads.at[i])
         for i, (src, dst) in enumerate(
             [
-                (x_hbm, x_ref), (d_hbm, d_ref), (pick_hbm, pick_ref), (key_hbm, keyrow_ref),
+                (x_hbm, x_ref), (d_hbm, d_ref), (key_hbm, keyrow_ref),
                 (fs_hbm, fs_ref), (sr_hbm, sr_ref), (metric_hbm, metric_ref),
                 (dh_hbm, dh_ref), (dl_hbm, dl_ref), (lift_hbm, lift_ref),
             ]
@@ -191,7 +191,22 @@
     sign = jnp.where(first, -1.0, 1.0)
     flayer = lax.rem(fl, half) // 32
     fnode = lax.rem(fl, 32)
-    fpad = jnp.where(fnode >= 25, 1.0, 0.0)
+
+    fside = jnp.where(first, 0, 1)
+    outer, inner = fnode // 5, lax.rem(fnode, 5)
+    nodes = [
+        jnp.broadcast_to(jnp.where(fnode < 25, at, 127), (C, FW))
+        for at in (100 * fside + fnode, 25 * outer + 20 * fside + inner, 5 * fnode + 4 * fside)
+    ]
+
+    def trace(volume, a):
+        value = None
+        for l in range(L):
+            part = jnp.take_along_axis(
+                volume[:, 128 * l : 128 * (l + 1)], nodes[a], axis=1, mode="promise_in_bounds"
+            )
+            value = part if value is None else jnp.where(flayer == l, part, value)
+        return value
 
     def roll(x, shift):
         shift = shift % FW
@@ -212,7 +227,7 @@
                 pad = 1.0 if pt == 0 and m % 4 == 0 else 0.0
                 u[pt, m, :, 128 * l + 120 : 128 * (l + 1)] = jnp.full((C, 8), pad, F32)
                 u[pt, m, :, 128 * l : 128 * l + 125] = ref[:, l, 125 * m : 125 * (m + 1)]
-    for copy in inputs[2:7]:
+    for copy in inputs[2:6]:
         copy.wait()
     keyrow = keyrow_ref[...].astype(F32)
     source = [column(fs_ref[f : f + 1, :].astype(F32)) for f in range(4)]
@@ -346,12 +361,10 @@
             put(0, m, 2, primal)
             put(1, m, 2, tangent)
 
-    whole = u[...].reshape(10 * C, VW)
-    for a in range(3):
-        faces = left(whole, pick_ref[a], 3).reshape(2, 5, C, FW)
-        for m in range(5):
-            uf[0, m, a] = faces[0, m] + fpad if m % 4 == 0 else faces[0, m]
-            uf[1, m, a] = faces[1, m]
+    for a in range(3):
+        for pt in range(2):
+            for m in range(5):
+                uf[pt, m, a] = trace(u[pt, m], a)
     blocks1, table1, sent1, zcopies1 = exchange(
         lambda pt, m, a: uf[pt, m, a], 5, sb1, rb1, zs1, zr1, 0
     )
@@ -369,7 +382,7 @@
         mv[a] = wide
         mf[a] = face
 
-    for copy in inputs[7:]:
+    for copy in inputs[6:]:
         copy.wait()
 
     own1 = sum(dot(hot_own, p) for p in table1[::-1])
@@ -432,7 +445,9 @@
                 v[a, 1, m, rows, :] = vt[a][m]
 
     for a in range(3):
-        vf[a] = left(v[a].reshape(8 * C, VW), pick_ref[a], 3).reshape(2, 4, C, FW)
+        for pt in range(2):
+            for m in range(4):
+                vf[a, pt, m] = trace(v[a, pt, m], a)
     blocks2, table2, sent2, zcopies2 = exchange(
         lambda pt, m, a: vf[a, pt, m], 4, sb2, rb2, zs2, zr2, 4
     )
@@ -522,37 +537,19 @@
     for copy in copies:
         copy.start()
     sta[0] = st[...]
-    writes = []
-    for pt, (part, out) in enumerate([(res, res_hbm), (prod, prod_hbm)]):
+    own_ref[...] = d_ref[...]
+    for pt, part in enumerate((res_ref, prod_ref)):
         for l in range(L):
             for m in range(5):
                 part[:, l, 125 * m : 125 * (m + 1)] = r[pt, m, :, 128 * l : 128 * l + 125]
-        writes.append(pltpu.make_async_copy(part, out, store.at[pt]))
-        writes[pt].start()
     for copy in copies:
         copy.wait()
     table_ref[...] = sta[...].reshape(everyone, 128)
-    for copy in writes:
-        copy.wait()
-
-
-def finish(
-    total_count, part_hbm, prod_hbm, d_hbm, table_hbm, res_hbm, basis_hbm, kry_ref,
-    res, prod, d, table_ref, basis, sems,
-):
-    loads = [
-        pltpu.make_async_copy(src, dst, sems.at[i])
-        for i, (src, dst) in enumerate(
-            [(part_hbm, res), (table_hbm, table_ref), (d_hbm, d), (prod_hbm, prod)]
-        )
-    ]
-    for copy in loads:
-        copy.start()
-    loads[0].wait()
-    first = pltpu.make_async_copy(res, res_hbm, sems.at[4])
+
+
+def finish(total_count, res, prod, d, table_ref, res_hbm, basis_hbm, kry_ref, basis, sems):
+    first = pltpu.make_async_copy(res, res_hbm, sems.at[0])
     first.start()
-    for copy in loads[1:]:
-        copy.wait()
     lane = lax.broadcasted_iota(jnp.int32, (1, 128), 1)
     table = table_ref[...]
     pd, dd, rs, rr, rd = [
@@ -568,7 +565,7 @@
     kry_ref[...] = row[0, :3]
     c, inv = coefficient, 1.0 / beta
     basis[...] = (prod[...] - c[:, :, None] * d[...]) * inv[:, :, None]
-    second = pltpu.make_async_copy(basis, basis_hbm, sems.at[5])
+    second = pltpu.make_async_copy(basis, basis_hbm, sems.at[1])
     second.start()
     first.wait()
     second.wait()
@@ -586,23 +583,23 @@
     keys[0, own : own + slots] = own + np.arange(slots)
     keys[0, own + SP : own + SP + slots] = own + slots + np.arange(slots)
     tiles = 4 * (slots // 8) + -(-4 * (slots % 8) // 8)
-    high, low, pick, lift = operators(L)
+    high, low, lift = operators(L)
     operands = (
         state, direction, jnp.transpose(metric, (2, 1, 0)), face_source.T, send_rows,
-        *[jnp.asarray(x) for x in (keys, high, low, pick, lift)],
+        *[jnp.asarray(x) for x in (keys, high, low, lift)],
     )
+    operands = [pltpu.with_memory_space_constraint(x, pltpu.HBM) for x in operands]
     vmem = lambda *shape: pltpu.VMEM(shape, F32)
     dma = lambda n: pltpu.SemaphoreType.DMA((n,))
     spec = pl.BlockSpec(memory_space=pltpu.VMEM)
-    parts, product, table = pl.pallas_call(
+    parts, product, own, table = pl.pallas_call(
         functools.partial(kernel, ns, np_),
         out_shape=(
-            jax.ShapeDtypeStruct(state.shape, F32),
-            jax.ShapeDtypeStruct(state.shape, F32),
+            *[jax.ShapeDtypeStruct(state.shape, F32)] * 3,
             jax.ShapeDtypeStruct((ns * np_, 128), F32),
         ),
-        in_specs=[pl.BlockSpec(memory_space=pltpu.HBM)] * 10,
-        out_specs=(pl.BlockSpec(memory_space=pltpu.HBM),) * 2 + (spec,),
+        in_specs=[pl.BlockSpec(memory_space=pltpu.HBM)] * 9,
+        out_specs=(spec,) * 4,
         scratch_shapes=[
             vmem(2, 5, C, VW), vmem(2, 5, 3, C, FW), vmem(2, 5, 3, C, FW),
             vmem(2, 4, C, VW), vmem(3, 2, 4, C, FW), vmem(3, 2, 4, C, VW),
@@ -613,10 +610,10 @@
             vmem(2, tiles, 8, FW), vmem(2, tiles, 8, FW), vmem(2, C, 2 * FW), vmem(2, C, 2 * FW),
             vmem(1, 128), vmem(ns * np_, 1, 128),
             *[pltpu.VMEM(x.shape, x.dtype) for x in operands],
-            dma(8), dma(8), dma(ns * np_), dma(ns * np_), dma(10), dma(2), vmem(C, L, width), vmem(C, L, width),
+            dma(8), dma(8), dma(ns * np_), dma(ns * np_), dma(9),
         ],
         compiler_params=pltpu.CompilerParams(
-            collective_id=0, has_side_effects=True, vmem_limit_bytes=63 * 1024 * 1024
+            collective_id=0, has_side_effects=True, vmem_limit_bytes=40 * 1024 * 1024
         ),
         name="navier",
     )(*operands)
@@ -628,15 +625,12 @@
             jax.ShapeDtypeStruct(state.shape, F32),
             jax.ShapeDtypeStruct((3,), F32),
         ),
-        in_specs=[hbm] * 4,
+        in_specs=[spec] * 4,
         out_specs=(hbm, hbm, spec),
-        scratch_shapes=[
-            vmem(C, L, width), vmem(C, L, width), vmem(C, L, width), vmem(ns * np_, 128),
-            vmem(C, L, width), dma(6),
-        ],
-        compiler_params=pltpu.CompilerParams(vmem_limit_bytes=63 * 1024 * 1024),
+        scratch_shapes=[vmem(C, L, width), dma(2)],
+        compiler_params=pltpu.CompilerParams(vmem_limit_bytes=16 * 1024 * 1024),
         name="finish",
-    )(parts, product, direction, table)
+    )(parts, product, own, table)
 
 
 def solution(mesh):

time: 29.8 us -> 27.3 us (0.916)
  Pallas kernels: 29 us -> 26.5 us
    pallas_call x1, Pallas kernels: 26.5 us -> 25.1 us  [local(): pl.pallas_call(functools.partial(kernel, ns, np_), out_shape=(*[jax.Shape...]
    pallas_call x1, Pallas kernels: 2.54 us -> 1.37 us  [local(): pl.pallas_call(functools.partial(finish, float(state.size * ns * np_)), o...]
where the time goes in v1:
time: 27.3 us; the launch traced here: 27.1 us
  Pallas kernels  26.5 us (97%)
  between operations  0.64 us (2%)
    pallas_call x1, Pallas kernels, local(): pl.pallas_call(functools.partial(kernel, ns, np_), out_shape=(*[jax.Shape...  25.1 us
    pallas_call x1, Pallas kernels, local(): pl.pallas_call(functools.partial(finish, float(state.size * ns * np_)), o...  1.37 us

profile of v1, /device:TPU:0, one launch (start us, length us, event | category | flops | bytes accessed | tf_op | source)
XLA Modules:
  0.0 27.1 jit_solution(14000154309741556267)
XLA Ops:
  0.6 25.1 %navier.1 = (f32[40,2,625]{2,1,0:T(2,128)S(1)}, f32[40,2,625]{2,1,0:T(2,128)S(1)}, f32[40,2,625]{2,1,0:T(2,128)S(1)}, f32[32,128]{1,0:T(8,128)S(1)}) custom-call(f32[40,2,625]{2,1,0:T(2,128)} %x_hbm.1, f32[40,2,625]{2,1,0:T(2,128)} %d_hbm.1, f32[3,2,40]{2,1,0:T(2,128)} %bitcast.2, s32[4,40]{1,0:T(4,128)} %bitcast.3, s32[1,2,33]{2,1,0:T(2,128)} %sr_hbm.1, ...), custom_call_target="tpu_custom_call" | custom-call | tf_op jit(solution)/shard_map/navier/pallas_call | solution.py:595
  25.8 1.4 %finish.1 = (f32[40,2,625]{2,1,0:T(2,128)}, f32[40,2,625]{2,1,0:T(2,128)}, f32[3]{0:T(128)}) custom-call(f32[40,2,625]{2,1,0:T(2,128)S(1)} %get-tuple-element.7.res, f32[40,2,625]{2,1,0:T(2,128)S(1)} %get-tuple-element.8.prod, f32[40,2,625]{2,1,0:T(2,128)S(1)} %get-tuple-element.9.d, f32[32,128]{1,0:T(8,128)S(1)} %get-tuple-element.10.table_ref), custom_call_target="tpu_custom_call" | custom-call | tf_op jit(solution)/shard_map/finish/pallas_call | solution.py:621

commit v2 on v1

v2 whole, which is shorter than its diff:
```python
import functools
import math

import jax
import jax.numpy as jnp
import numpy as np
from jax import lax
from jax.experimental import pallas as pl
from jax.experimental.pallas import tpu as pltpu
from jax.sharding import PartitionSpec as P

GAMMA = 1.4
VISC = 0.01
COND = VISC * GAMMA / ((GAMMA - 1.0) * 0.72)
LIFT = 10.0
MESH = pl.DeviceIdType.MESH
F32, BF16 = jnp.float32, jnp.bfloat16


def diff_table():
    spread = math.sqrt(3.0 / 7.0)
    points = np.array([-1.0, -spread, 0.0, spread, 1.0])
    weights = np.array(
        [np.prod([points[i] - points[j] for j in range(5) if j != i]) for i in range(5)]
    )
    matrix = np.zeros((5, 5))
    for i in range(5):
        for j in range(5):
            if i != j:
                matrix[i, j] = weights[i] / (weights[j] * (points[i] - points[j]))
        matrix[i, i] = np.sum([1.0 / (points[i] - points[j]) for j in range(5) if j != i])
    return matrix


def operators(layers):
    table = diff_table()
    eye = np.eye(5)
    kron = [
        np.einsum("ai,bj,ck->ijkabc", *[table if m == a else eye for m in range(3)]).reshape(125, 125)
        for a in range(3)
    ]
    node = np.arange(125).reshape(5, 5, 5)
    vw, fw, half = 128 * layers, 64 * layers, 32 * layers
    deriv = np.zeros((3, vw, vw), np.float32)
    pick = np.zeros((3, vw, fw), np.float32)
    for a in range(3):
        for l in range(layers):
            b = 128 * l
            deriv[a, b : b + 125, b : b + 125] = kron[a]
            for side in range(2):
                face = np.take(node, 4 * side, axis=a).reshape(-1)
                for m, at in enumerate(face):
                    pick[a, b + at, side * half + 32 * l + m] = 1.0
    high = deriv.astype(jnp.bfloat16)
    low = (deriv - high.astype(np.float32)).astype(jnp.bfloat16)
    lift = np.swapaxes(pick, 1, 2).astype(jnp.bfloat16)
    return np.concatenate([low, high, lift], axis=1)


def pieces(x, n):
    out = []
    for i in range(n):
        p = x.astype(BF16)
        out.append(p)
        if i + 1 < n:
            x = x - p.astype(F32)
    return out


def dot(a, b):
    return jnp.dot(a, b, preferred_element_type=F32)


def fields_of(u):
    inv = 1.0 / u[0]
    vel = [u[1] * inv, u[2] * inv, u[3] * inv]
    kinetic = 0.5 * (u[1] * vel[0] + u[2] * vel[1] + u[3] * vel[2])
    pressure = (GAMMA - 1.0) * (u[4] - kinetic)
    return vel, pressure, pressure * inv


def inviscid(u, a):
    vel, pressure, _ = fields_of(u)
    out = [u[1 + a]]
    for m in range(3):
        term = u[1 + m] * vel[a]
        out.append(term + pressure if m == a else term)
    out.append((u[4] + pressure) * vel[a])
    return out


def viscous(vel, q, a, divergence):
    stress = []
    for m in range(3):
        term = q[a][m] + q[m][a]
        if m == a:
            term = term - 2.0 / 3.0 * divergence
        stress.append(VISC * term)
    energy = stress[0] * vel[0] + stress[1] * vel[1] + stress[2] * vel[2] + COND * q[a][3]
    return stress + [energy]


def viscous_all(u, q):
    inv = 1.0 / u[0]
    vel = [u[1] * inv, u[2] * inv, u[3] * inv]
    divergence = q[0][0] + q[1][1] + q[2][2]
    return [viscous(vel, q, a, divergence) for a in range(3)]


def viscous_at(u, q, a):
    inv = 1.0 / u[0]
    vel = [u[1] * inv, u[2] * inv, u[3] * inv]
    return viscous(vel, q, a, q[0][0] + q[1][1] + q[2][2])


def gradient_fields(u):
    vel, _, temper = fields_of(u)
    return vel + [temper]


def jump_fields(inner, outer):
    return [o - i for o, i in zip(gradient_fields(outer), gradient_fields(inner))]


def surface(inner, outer, sign, a):
    vi, pi, ti = fields_of(inner)
    vo, po, to = fields_of(outer)
    square = sum(v * v for v in vi) + GAMMA * ti + sum(v * v for v in vo) + GAMMA * to
    speed = jnp.sqrt(0.5 * square)
    fi, fo = inviscid(inner, a), inviscid(outer, a)
    return [
        (0.5 * LIFT) * (sign * (fo[m] - fi[m]) - speed * (outer[m] - inner[m])) for m in range(5)
    ]


def ratio(top, bottom):
    return jnp.where(bottom > 0.0, top / jnp.where(bottom > 0.0, bottom, 1.0), 0.0)


def needed(a):
    return [(a, f) for f in range(4)] + [x for b in range(3) if b != a for x in ((b, a), (b, b))]


def kernel(
    ns, np_,
    x_hbm, d_hbm, metric_hbm, fs_hbm, sr_hbm, key_hbm, ops_hbm,
    res_ref, prod_ref, own_ref, table_ref,
    u, uf, of, w, jf, q, qf, vf, g, s, r, mv, mf,
    sb1, rb1, zs1, zr1, sb2, rb2, zs2, zr2, st, sta,
    xd, metric_ref, fs_ref, sr_ref, key_ref, ops_ref,
    xsend, xrecv, stsem, loads,
):
    C, L = xd.shape[1], xd.shape[2]
    VW, FW, half = 128 * L, 64 * L, 32 * L
    SLOTS = sr_ref.shape[2]
    SP = -(-SLOTS // 8) * 8
    MAIN, REM = SLOTS // 8, SLOTS % 8
    OWN = 4 * C
    ms, mp = lax.axis_index("stream"), lax.axis_index("span")
    lower, upper = lax.rem(ms + ns - 1, ns), lax.rem(ms + 1, ns)
    below, above = lax.rem(mp + np_ - 1, np_), lax.rem(mp + 1, np_)

    inputs = [
        pltpu.make_async_copy(src, dst, loads.at[i])
        for src, dst, i in [
            (x_hbm, xd.at[0], 0), (d_hbm, xd.at[1], 0), (key_hbm, key_ref, 1), (fs_hbm, fs_ref, 2),
            (sr_hbm, sr_ref, 3), (metric_hbm, metric_ref, 4), (ops_hbm, ops_ref, 5),
        ]
    ]
    for copy in inputs:
        copy.start()

    def peer(k):
        a, b = divmod(k, np_)
        return lax.rem(ms + a, ns), lax.rem(mp + b, np_)

    everyone = ns * np_
    barrier = pltpu.get_barrier_semaphore()
    for k in range(1, everyone):
        pl.semaphore_signal(barrier, inc=1, device_id=peer(k), device_id_type=MESH)

    fl = lax.broadcasted_iota(jnp.int32, (1, FW), 1)
    vl = lax.broadcasted_iota(jnp.int32, (1, VW), 1)
    first = fl < half
    sign = jnp.where(first, -1.0, 1.0)
    flayer = lax.rem(fl, half) // 32
    fnode = lax.rem(fl, 32)
    fside = jnp.where(first, 0, 1)
    major, minor = fnode // 5, lax.rem(fnode, 5)
    nodes = [
        jnp.where(fnode < 25, at, 127)
        for at in (100 * fside + fnode, 25 * major + 20 * fside + minor, 5 * fnode + 4 * fside)
    ]

    def pull(x, at):
        return jnp.take_along_axis(
            x, jnp.broadcast_to(at, x.shape), axis=1, mode="promise_in_bounds"
        )

    def trace(volume, a):
        value = None
        for l in range(L):
            part = pull(volume[:, 128 * l : 128 * (l + 1)], nodes[a])
            value = part if value is None else jnp.where(flayer == l, part, value)
        return value

    def edge(a, b):
        at = dict(zip([x for x in range(3) if x != a], (major, minor)))
        at[a] = 4 * fside
        one, two = [x for x in range(3) if x != b]
        there = (lax.rem(at[b], 4) == 0) & (fnode < 25)
        lane = half * (at[b] // 4) + 32 * flayer + 5 * at[one] + at[two]
        return there, jnp.where(there, lane, 0)

    edges = {(a, b): edge(a, b) for a in range(3) for b in range(3) if a != b}

    def roll(x, shift):
        shift = shift % FW
        return pltpu.roll(x, shift, 1) if shift else x

    di = lax.broadcasted_iota(jnp.int32, (C, C), 0)
    dj = lax.broadcasted_iota(jnp.int32, (C, C), 1)

    def column(row):
        return jnp.sum(jnp.where(di == dj, row, 0.0), axis=1, keepdims=True)

    def blocks_of(body):
        @pl.loop(0, C // 8, unroll=True)
        def _(i):
            body(pl.ds(pl.multiple_of(i * 8, 8), 8))

    def lift(axes, values):
        halves, table = [], []
        for a, value in zip(axes, values):
            halves += pieces(value, 2)
            table += [ops_ref[a, 2 * VW :]] * 2
        return dot(jnp.concatenate(halves, axis=1), jnp.concatenate(table, axis=0))

    def derive(axes, values):
        halves, table = [], []
        for a, value in zip(axes, values):
            high, low = pieces(value, 2)
            halves += [high, low, high]
            table += [ops_ref[a, : 2 * VW], ops_ref[a, VW : 2 * VW]]
        return dot(jnp.concatenate(halves, axis=1), jnp.concatenate(table, axis=0))

    def choose(hot, x):
        return dot(hot, jnp.concatenate(pieces(x, 3)[::-1], axis=0))

    def swap(a, b):
        return (
            jnp.where(first, a, pltpu.roll(b, half, 1)),
            jnp.where(first, pltpu.roll(a, half, 1), b),
        )

    def landed(ref, sem):
        pltpu.make_async_copy(ref, ref, sem).wait()

    def remote(pairs, base):
        for src, dst, to in pairs:
            pltpu.make_async_remote_copy(
                src_ref=src, dst_ref=dst, send_sem=xsend.at[base],
                recv_sem=xrecv.at[base], device_id=to, device_id_type=MESH,
            ).start()

    def arrived(source, target, base):
        landed(target, xrecv.at[base])
        landed(source, xsend.at[base])

    def plane_pack(faces, members, sb):
        blocks = [[swap(faces(0, m, a), faces(1, m, a)) for m in range(members)] for a in range(2)]
        table = jnp.concatenate(
            [
                jnp.concatenate([blocks[a][m][side] for m in range(members)], axis=1)
                for side in range(2)
                for a in range(2)
            ],
            axis=0,
        )
        sent = choose(send_hot, table)
        for m in range(4):
            value = sent[:, FW * m : FW * (m + 1)]
            if members > 4:
                spare = roll(sent[:, 4 * FW :], 25 - 7 * m)
                value = jnp.where(fnode < 25, value, spare)
            for side in range(2):
                for b in range(MAIN):
                    at = side * SP + 8 * b
                    sb[side, 4 * b + m] = value[at : at + 8]
                for e in range(REM):
                    at, to = side * SP + 8 * MAIN + e, REM * m + e
                    sb[side, 4 * MAIN + to // 8, to % 8 : to % 8 + 1, :] = value[at : at + 1]
        return table

    def plane_send(sb, rb, base):
        remote([(sb.at[0], rb.at[1], (lower, mp)), (sb.at[1], rb.at[0], (upper, mp))], base)

    def layer_send(faces, members, zs, zr, base):
        blocks = [swap(faces(0, m, 2), faces(1, m, 2)) for m in range(members)]
        for m in range(0, members, 2):
            for side in range(2):
                value = blocks[m][side]
                if m + 1 < members:
                    other = roll(blocks[m + 1][side], 32 if side == 0 else -32)
                    value = jnp.where(flayer == (0 if side == 0 else L - 1), value, other)
                zs[side, :, FW * (m // 2) : FW * (m // 2 + 1)] = value
        remote([(zs.at[0], zr.at[1], (ms, below)), (zs.at[1], zr.at[0], (ms, above))], base)
        return blocks

    def plane_outside(own, rb, members, put):
        row8 = lax.broadcasted_iota(jnp.int32, (8, 1), 0)
        rows = []
        for side in range(2):
            rows += [
                jnp.concatenate([rb[side, 4 * b + m] for m in range(4)], axis=1)
                for b in range(MAIN)
            ]
            if REM:
                parts = []
                for m in range(4):
                    part = jnp.zeros((8, FW), F32)
                    for e in range(REM):
                        to = REM * m + e
                        line = rb[side, 4 * MAIN + to // 8, to % 8 : to % 8 + 1, :]
                        part = jnp.where(row8 == e, line, part)
                    parts.append(part)
                rows.append(jnp.concatenate(parts, axis=1))
        received = jnp.concatenate(rows, axis=0)
        if members * FW > received.shape[1]:
            spare = jnp.zeros((2 * SP, FW), F32)
            for m in range(received.shape[1] // FW):
                part = roll(received[:, FW * m : FW * (m + 1)], 7 * m - 25)
                spare = jnp.where((fnode >= 7 * m) & (fnode < 7 * m + 7), part, spare)
            received = jnp.concatenate([received, spare], axis=1)
        got = own + choose(hot_recv, received)
        for a in range(2):
            for m in range(members):
                lanes = slice(FW * m, FW * (m + 1))
                lo = got[a * C : (a + 1) * C, lanes]
                hi = got[(2 + a) * C : (3 + a) * C, lanes]
                primal, tangent = swap(lo, hi)
                put(0, m, a, primal)
                put(1, m, a, tangent)

    def layer_outside(blocks, zr, members, put):
        for m in range(members):
            lanes = slice(FW * (m // 2), FW * (m // 2 + 1))
            step = 32 * (L - 1 if m % 2 == 0 else L - 2)
            lo = jnp.where(flayer == 0, roll(zr[0, :, lanes], -step), roll(blocks[m][1], 32))
            hi = jnp.where(flayer == L - 1, roll(zr[1, :, lanes], step), roll(blocks[m][0], -32))
            primal, tangent = swap(lo, hi)
            put(0, m, 2, primal)
            put(1, m, 2, tangent)

    landed(xd, loads.at[0])
    for pt in range(2):
        for l in range(L):
            for m in range(5):
                pad = 1.0 if pt == 0 and m % 4 == 0 else 0.0
                u[pt, m, :, 128 * l + 120 : 128 * (l + 1)] = jnp.full((C, 8), pad, F32)
                u[pt, m, :, 128 * l : 128 * l + 125] = xd[pt, :, l, 125 * m : 125 * (m + 1)]
    for copy in inputs[2:6]:
        copy.wait()
    own_keys, recv_keys = key_ref[0:1, : 3 * OWN], key_ref[1:2, : 6 * SP]
    source = [column(fs_ref[f : f + 1, :].astype(F32)) for f in range(4)]

    def hot(keys):
        rows = [jnp.where(source[2 * a + side] == keys, 1.0, 0.0) for side in range(2) for a in range(2)]
        return jnp.concatenate(rows, axis=0).astype(BF16)

    hot_own, hot_recv = hot(own_keys), hot(recv_keys)
    ri = lax.broadcasted_iota(jnp.int32, (SP, SLOTS), 0)
    li = lax.broadcasted_iota(jnp.int32, (SP, SLOTS), 1)
    send_hot = []
    for side in range(2):
        row = sr_ref[0, side : side + 1, :].astype(F32)
        wanted = jnp.sum(jnp.where(ri == li, row, 0.0), axis=1, keepdims=True)
        send_hot.append(jnp.where(wanted == own_keys, 1.0, 0.0))
    send_hot = jnp.concatenate(send_hot, axis=0).astype(BF16)

    def state_faces(a):
        for pt in range(2):
            for m in range(5):
                uf[pt, m, a] = trace(u[pt, m], a)

    state_faces(0)
    state_faces(1)
    table1 = plane_pack(lambda pt, m, a: uf[pt, m, a], 5, sb1)
    pl.semaphore_wait(barrier, everyone - 1)
    plane_send(sb1, rb1, 0)
    state_faces(2)
    blocks1 = layer_send(lambda pt, m, a: uf[pt, m, a], 5, zs1, zr1, 1)

    for a in range(3):
        wide = jnp.zeros((C, VW), F32)
        face = jnp.zeros((C, FW), F32)
        for l in range(L):
            value = column(metric_ref[a, l : l + 1, :])
            wide = jnp.where(vl // 128 == l, value, wide)
            face = jnp.where(flayer == l, value, face)
        mv[a] = wide
        mf[a] = face

    def gradients(rows):
        primal = [u[0, m, rows, :] for m in range(5)]
        tangent = [u[1, m, rows, :] for m in range(5)]
        fp, ft = jax.jvp(gradient_fields, (primal,), (tangent,))
        for m in range(4):
            w[0, m, rows, :] = fp[m]
            w[1, m, rows, :] = ft[m]

    blocks_of(gradients)
    inputs[6].wait()
    own1 = choose(hot_own, table1)
    fields = w[...].reshape(8 * C, VW)
    for a in range(3):
        q[a] = derive([a], [fields]).reshape(2, 4, C, VW)
    for a in range(3):
        for pt in range(2):
            for n, (b, f) in enumerate(needed(a)):
                qf[a, pt, n] = trace(q[b, pt, f], a)

    low_wall = jnp.where(source[2] < 0.0, 1.0, 0.0)
    high_wall = jnp.where(source[3] < 0.0, 1.0, 0.0)
    wall = jnp.where(first, low_wall, high_wall) > 0.5

    def put1(pt, m, a, value):
        if a == 1:
            own = uf[pt, m, a]
            value = jnp.where(wall, own if m % 4 == 0 else -own, value)
        of[pt, m, a] = jnp.where(fnode < 25, value, uf[pt, m, a])

    def jumps(a):
        def body(rows):
            primal = ([uf[0, m, a, rows, :] for m in range(5)], [of[0, m, a, rows, :] for m in range(5)])
            tangent = ([uf[1, m, a, rows, :] for m in range(5)], [of[1, m, a, rows, :] for m in range(5)])
            jp, jt = jax.jvp(jump_fields, primal, tangent)
            for m in range(4):
                jf[a, 0, m, rows, :] = (0.5 * LIFT) * sign * jp[m]
                jf[a, 1, m, rows, :] = (0.5 * LIFT) * sign * jt[m]

        blocks_of(body)

    def edge_jumps(a, b):
        there, lane = edges[a, b]
        for n, (other, f) in enumerate(needed(a)):
            if other == b:
                for pt in range(2):
                    qf[a, pt, n] += jnp.where(there, pull(jf[b, pt, f], lane), 0.0)

    arrived(zs1, zr1, 1)
    layer_outside(blocks1, zr1, 5, put1)
    jumps(2)
    edge_jumps(0, 2)
    edge_jumps(1, 2)
    arrived(sb1, rb1, 0)
    plane_outside(own1, rb1, 5, put1)
    jumps(0)
    jumps(1)
    edge_jumps(0, 1)
    edge_jumps(1, 0)

    def face_viscous(a):
        def body(rows):
            states = [[uf[pt, m, a, rows, :] for m in range(5)] for pt in range(2)]
            grads = []
            for pt in range(2):
                grad = [[None] * 4 for _ in range(3)]
                for n, (b, f) in enumerate(needed(a)):
                    value = qf[a, pt, n, rows, :]
                    if b == a:
                        value = value + jf[a, pt, f, rows, :]
                    grad[b][f] = mf[b, rows, :] * value
                grads.append(grad)
            vp, vt = jax.jvp(
                lambda x, y: viscous_at(x, y, a), (states[0], grads[0]), (states[1], grads[1])
            )
            for m in range(4):
                vf[a, 0, m, rows, :] = vp[m]
                vf[a, 1, m, rows, :] = vt[m]

        blocks_of(body)

    face_viscous(0)
    face_viscous(1)
    table2 = plane_pack(lambda pt, m, a: vf[a, pt, m], 4, sb2)
    plane_send(sb2, rb2, 2)
    edge_jumps(2, 0)
    edge_jumps(2, 1)
    face_viscous(2)
    blocks2 = layer_send(lambda pt, m, a: vf[a, pt, m], 4, zs2, zr2, 3)

    own2 = choose(hot_own, table2)
    for a in range(3):
        q[a] += lift([a], [jf[a].reshape(8 * C, FW)]).reshape(2, 4, C, VW)

    def fluxes(rows):
        scale = [mv[a, rows, :] for a in range(3)]
        states = [[u[pt, m, rows, :] for m in range(5)] for pt in range(2)]
        grads = [
            [[scale[a] * q[a, pt, m, rows, :] for m in range(4)] for a in range(3)]
            for pt in range(2)
        ]
        visc = jax.jvp(viscous_all, (states[0], grads[0]), (states[1], grads[1]))
        for a in range(3):
            euler = jax.jvp(lambda x: inviscid(x, a), (states[0],), (states[1],))
            for pt in range(2):
                g[a, pt, 0, rows, :] = scale[a] * euler[pt][0]
                for m in range(4):
                    g[a, pt, m + 1, rows, :] = scale[a] * (euler[pt][m + 1] - visc[pt][a][m])

    blocks_of(fluxes)
    for a in range(3):
        def surfaces(rows):
            primal = ([uf[0, m, a, rows, :] for m in range(5)], [of[0, m, a, rows, :] for m in range(5)])
            tangent = ([uf[1, m, a, rows, :] for m in range(5)], [of[1, m, a, rows, :] for m in range(5)])
            both = jax.jvp(
                lambda inner, outer: surface(inner, outer, sign, a), primal, tangent
            )
            scale = mf[a, rows, :]
            for pt in range(2):
                s[a, pt, 0, rows, :] = scale * both[pt][0]
                for m in range(4):
                    mine = (0.5 * LIFT) * sign * vf[a, pt, m, rows, :]
                    s[a, pt, m + 1, rows, :] = scale * (both[pt][m + 1] + mine)

        blocks_of(surfaces)

    total = derive(range(3), [g[a].reshape(10 * C, VW) for a in range(3)])
    total += lift(range(3), [s[a].reshape(10 * C, FW) for a in range(3)])
    r[...] = total.reshape(2, 5, C, VW)

    def whole_sum(parts):
        acc = parts[0]
        for part in parts[1:]:
            acc = acc + part
        return jnp.sum(jnp.sum(acc, axis=0, keepdims=True), axis=1, keepdims=True)

    pd = whole_sum([r[1, m] * u[1, m] for m in range(5)])
    dd = whole_sum([u[1, m] * u[1, m] for m in range(5)])
    mine = ratio(pd, dd)

    def put2(pt, m, a, value):
        if a == 1:
            value = jnp.where(wall, vf[a, pt, m], value)
        s[a, pt, m] = (-0.5 * LIFT) * sign * mf[a] * value

    arrived(zs2, zr2, 3)
    layer_outside(blocks2, zr2, 4, put2)

    arrived(sb2, rb2, 2)
    plane_outside(own2, rb2, 4, put2)
    lifted = lift(range(3), [s[a, :, :4].reshape(8 * C, FW) for a in range(3)])
    lifted = lifted.reshape(2, 4, C, VW)
    for pt in range(2):
        r[pt, 1:] += lifted[pt]
    rests = [r[1, m] - mine * u[1, m] for m in range(5)]
    rs = whole_sum([r[0, m] * r[0, m] for m in range(5)])
    rr = whole_sum([x * x for x in rests])
    rd = whole_sum([x * u[1, m] for m, x in enumerate(rests)])
    lane = lax.broadcasted_iota(jnp.int32, (1, 128), 1)
    row = jnp.zeros((1, 128), F32)
    for i, value in enumerate((mine, dd, rs, rr, rd)):
        row = jnp.where(lane == i, value, row)
    st[...] = row
    for k in range(1, everyone):
        pltpu.make_async_remote_copy(
            src_ref=st, dst_ref=sta.at[k], send_sem=stsem.at[0], recv_sem=stsem.at[1],
            device_id=peer(k), device_id_type=MESH,
        ).start()
    sta[0] = st[...]
    own_ref[...] = xd[1]
    for pt, part in enumerate((res_ref, prod_ref)):
        for l in range(L):
            for m in range(5):
                part[:, l, 125 * m : 125 * (m + 1)] = r[pt, m, :, 128 * l : 128 * l + 125]
    landed(sta.at[pl.ds(1, everyone - 1)], stsem.at[1])
    landed(sta.at[pl.ds(1, everyone - 1)], stsem.at[0])
    table_ref[...] = sta[...].reshape(everyone, 128)


def finish(total_count, res, prod, d, table_ref, res_hbm, basis_hbm, kry_ref, basis, sems):
    first = pltpu.make_async_copy(res, res_hbm, sems.at[0])
    first.start()
    lane = lax.broadcasted_iota(jnp.int32, (1, 128), 1)
    table = table_ref[...]
    mine, dd, rs, rr, rd = [
        jnp.sum(jnp.where(lane == i, table, 0.0), axis=1, keepdims=True) for i in range(5)
    ]
    coefficient = jnp.sum(rd + mine * dd, axis=0, keepdims=True) * (1.0 / total_count)
    shift = mine - coefficient
    rr = jnp.sum(rr + 2.0 * shift * rd + shift * shift * dd, axis=0, keepdims=True)
    rs = jnp.sum(rs, axis=0, keepdims=True)
    beta = jnp.sqrt(rr * (1.0 / total_count))
    norm = jnp.sqrt(rs * (1.0 / total_count))
    row = jnp.where(lane == 0, coefficient, jnp.where(lane == 1, beta, norm))
    kry_ref[...] = row[0, :3]
    c, inv = coefficient, 1.0 / beta
    basis[...] = (prod[...] - c[:, :, None] * d[...]) * inv[:, :, None]
    second = pltpu.make_async_copy(basis, basis_hbm, sems.at[1])
    second.start()
    first.wait()
    second.wait()


def local(ns, np_, state, direction, metric, face_source, send_rows):
    C, L, width = state.shape
    slots = send_rows.shape[2]
    SP = -(-slots // 8) * 8
    VW, FW = 128 * L, 64 * L
    own = 4 * C
    keys = np.full((2, max(3 * own, 6 * SP)), -7, np.float32)
    side, rest = np.divmod(np.arange(own), 2 * C)
    keys[0, : 3 * own] = np.tile(4 * (rest % C) + 2 * (rest // C) + side, 3)
    for copy in range(3):
        for side in range(2):
            at = (2 * copy + side) * SP
            keys[1, at : at + slots] = own + side * slots + np.arange(slots)
    tiles = 4 * (slots // 8) + -(-4 * (slots % 8) // 8)
    operands = (
        state, direction, jnp.transpose(metric, (2, 1, 0)), face_source.T, send_rows,
        jnp.asarray(keys), jnp.asarray(operators(L)),
    )
    operands = [pltpu.with_memory_space_constraint(x, pltpu.HBM) for x in operands]
    vmem = lambda *shape: pltpu.VMEM(shape, F32)
    dma = lambda n: pltpu.SemaphoreType.DMA((n,))
    spec = pl.BlockSpec(memory_space=pltpu.VMEM)
    parts, product, own, table = pl.pallas_call(
        functools.partial(kernel, ns, np_),
        out_shape=(
            *[jax.ShapeDtypeStruct(state.shape, F32)] * 3,
            jax.ShapeDtypeStruct((ns * np_, 128), F32),
        ),
        in_specs=[pl.BlockSpec(memory_space=pltpu.HBM)] * 7,
        out_specs=(spec,) * 4,
        scratch_shapes=[
            vmem(2, 5, C, VW), vmem(2, 5, 3, C, FW), vmem(2, 5, 3, C, FW),
            vmem(2, 4, C, VW), vmem(3, 2, 4, C, FW), vmem(3, 2, 4, C, VW),
            vmem(3, 2, 8, C, FW), vmem(3, 2, 4, C, FW),
            vmem(3, 2, 5, C, VW), vmem(3, 2, 5, C, FW), vmem(2, 5, C, VW),
            vmem(3, C, VW), vmem(3, C, FW),
            vmem(2, tiles, 8, FW), vmem(2, tiles, 8, FW), vmem(2, C, 3 * FW), vmem(2, C, 3 * FW),
            vmem(2, tiles, 8, FW), vmem(2, tiles, 8, FW), vmem(2, C, 2 * FW), vmem(2, C, 2 * FW),
            vmem(1, 128), vmem(ns * np_, 1, 128),
            vmem(2, C, L, width), *[pltpu.VMEM(x.shape, x.dtype) for x in operands[2:]],
            dma(4), dma(4), dma(2), dma(6),
        ],
        compiler_params=pltpu.CompilerParams(
            collective_id=0, has_side_effects=True, vmem_limit_bytes=40 * 1024 * 1024
        ),
        name="navier",
    )(*operands)
    hbm = pl.BlockSpec(memory_space=pltpu.HBM)
    return pl.pallas_call(
        functools.partial(finish, float(state.size * ns * np_)),
        out_shape=(
            jax.ShapeDtypeStruct(state.shape, F32),
            jax.ShapeDtypeStruct(state.shape, F32),
            jax.ShapeDtypeStruct((3,), F32),
        ),
        in_specs=[spec] * 4,
        out_specs=(hbm, hbm, spec),
        scratch_shapes=[vmem(C, L, width), dma(2)],
        compiler_params=pltpu.CompilerParams(vmem_limit_bytes=16 * 1024 * 1024),
        name="finish",
    )(parts, product, own, table)


def solution(mesh):
    return jax.shard_map(
        functools.partial(local, mesh.shape["stream"], mesh.shape["span"]),
        mesh=mesh,
        in_specs=(
            P("stream", "span", None),
            P("stream", "span", None),
            P("stream", "span", None),
            P("stream", None),
            P("stream", None, None),
        ),
        out_specs=(P("stream", "span", None), P("stream", "span", None), P()),
        check_vma=False,
    )
```

time: 27.3 us -> 25.2 us (0.923)
  Pallas kernels: 26.5 us -> 24.4 us
    pallas_call x1, Pallas kernels: 25.1 us -> 23.1 us  [local(): pl.pallas_call(functools.partial(kernel, ns, np_), out_shape=(*[jax.Shape...]
where the time goes in v2:
time: 25.2 us; the launch traced here: 25.1 us
  Pallas kernels  24.4 us (97%)
  between operations  0.64 us (3%)
    pallas_call x1, Pallas kernels, local(): pl.pallas_call(functools.partial(kernel, ns, np_), out_shape=(*[jax.Shape...  23.1 us
    pallas_call x1, Pallas kernels, local(): pl.pallas_call(functools.partial(finish, float(state.size * ns * np_)), o...  1.38 us

profile of v2, /device:TPU:0, one launch (start us, length us, event | category | flops | bytes accessed | tf_op | source)
XLA Modules:
  0.0 25.1 jit_solution(3742002596146138420)
XLA Ops:
  0.6 23.1 %navier.1 = (f32[40,2,625]{2,1,0:T(2,128)S(1)}, f32[40,2,625]{2,1,0:T(2,128)S(1)}, f32[40,2,625]{2,1,0:T(2,128)S(1)}, f32[32,128]{1,0:T(8,128)S(1)}) custom-call(f32[40,2,625]{2,1,0:T(2,128)} %x_hbm.1, f32[40,2,625]{2,1,0:T(2,128)} %d_hbm.1, f32[3,2,40]{2,1,0:T(2,128)} %bitcast.2, s32[4,40]{1,0:T(4,128)} %bitcast.3, s32[1,2,33]{2,1,0:T(2,128)} %sr_hbm.1, ...), custom_call_target="tpu_custom_call" | custom-call | tf_op jit(solution)/shard_map/navier/pallas_call | solution.py:628
  23.7 1.4 %finish.1 = (f32[40,2,625]{2,1,0:T(2,128)}, f32[40,2,625]{2,1,0:T(2,128)}, f32[3]{0:T(128)}) custom-call(f32[40,2,625]{2,1,0:T(2,128)S(1)} %get-tuple-element.7.res, f32[40,2,625]{2,1,0:T(2,128)S(1)} %get-tuple-element.8.prod, f32[40,2,625]{2,1,0:T(2,128)S(1)} %get-tuple-element.9.d, f32[32,128]{1,0:T(8,128)S(1)} %get-tuple-element.10.table_ref), custom_call_target="tpu_custom_call" | custom-call | tf_op jit(solution)/shard_map/finish/pallas_call | solution.py:654

commit v3 on v2

--- a/solution.py
+++ b/solution.py
@@ -118,10 +118,6 @@
     return vel + [temper]
 
 
-def jump_fields(inner, outer):
-    return [o - i for o, i in zip(gradient_fields(outer), gradient_fields(inner))]
-
-
 def surface(inner, outer, sign, a):
     vi, pi, ti = fields_of(inner)
     vo, po, to = fields_of(outer)
@@ -148,7 +144,7 @@
     u, uf, of, w, jf, q, qf, vf, g, s, r, mv, mf,
     sb1, rb1, zs1, zr1, sb2, rb2, zs2, zr2, st, sta,
     xd, metric_ref, fs_ref, sr_ref, key_ref, ops_ref,
-    xsend, xrecv, stsem, loads,
+    xsend, xrecv, stsem, loads, word,
 ):
     C, L = xd.shape[1], xd.shape[2]
     VW, FW, half = 128 * L, 64 * L, 32 * L
@@ -175,9 +171,22 @@
         return lax.rem(ms + a, ns), lax.rem(mp + b, np_)
 
     everyone = ns * np_
+    rounds = 4 if ns == 8 else 0
+    near = [np_, everyone - np_, *range(1, np_)]
+    greeted = near if rounds else list(range(1, everyone))
     barrier = pltpu.get_barrier_semaphore()
-    for k in range(1, everyone):
+    for k in greeted:
         pl.semaphore_signal(barrier, inc=1, device_id=peer(k), device_id_type=MESH)
+
+    def pass_on(i):
+        for side, to in ((0, lower), (1, upper)):
+            if i > 0:
+                pl.semaphore_wait(word.at[i - 1, side], 1)
+        if i < rounds:
+            for side, to in ((0, lower), (1, upper)):
+                pl.semaphore_signal(
+                    word.at[i, 1 - side], inc=1, device_id=(to, mp), device_id_type=MESH
+                )
 
     fl = lax.broadcasted_iota(jnp.int32, (1, FW), 1)
     vl = lax.broadcasted_iota(jnp.int32, (1, VW), 1)
@@ -244,8 +253,8 @@
             table += [ops_ref[a, : 2 * VW], ops_ref[a, VW : 2 * VW]]
         return dot(jnp.concatenate(halves, axis=1), jnp.concatenate(table, axis=0))
 
-    def choose(hot, x):
-        return dot(hot, jnp.concatenate(pieces(x, 3)[::-1], axis=0))
+    def choose(hot, x, depth=3):
+        return dot(hot[:, : depth * x.shape[0]], jnp.concatenate(pieces(x, depth)[::-1], axis=0))
 
     def swap(a, b):
         return (
@@ -307,7 +316,9 @@
         remote([(zs.at[0], zr.at[1], (ms, below)), (zs.at[1], zr.at[0], (ms, above))], base)
         return blocks
 
-    def plane_outside(own, rb, members, put):
+    def plane_outside(own, rb, members, put, depth):
+        lanes = lax.broadcasted_iota(jnp.int32, (1, members * FW), 1)
+        member, node = lanes // FW, lax.rem(lanes, 32)
         row8 = lax.broadcasted_iota(jnp.int32, (8, 1), 0)
         rows = []
         for side in range(2):
@@ -332,7 +343,9 @@
                 part = roll(received[:, FW * m : FW * (m + 1)], 7 * m - 25)
                 spare = jnp.where((fnode >= 7 * m) & (fnode < 7 * m + 7), part, spare)
             received = jnp.concatenate([received, spare], axis=1)
-        got = own + choose(hot_recv, received)
+            pad = jnp.where(lax.rem(member, 4) == 0, 1.0, 0.0)
+            received = jnp.where(node < 25, received, pad)
+        got = own + choose(hot_recv, received, depth)
         for a in range(2):
             for m in range(members):
                 lanes = slice(FW * m, FW * (m + 1))
@@ -362,13 +375,6 @@
     for copy in inputs[2:6]:
         copy.wait()
     own_keys, recv_keys = key_ref[0:1, : 3 * OWN], key_ref[1:2, : 6 * SP]
-    source = [column(fs_ref[f : f + 1, :].astype(F32)) for f in range(4)]
-
-    def hot(keys):
-        rows = [jnp.where(source[2 * a + side] == keys, 1.0, 0.0) for side in range(2) for a in range(2)]
-        return jnp.concatenate(rows, axis=0).astype(BF16)
-
-    hot_own, hot_recv = hot(own_keys), hot(recv_keys)
     ri = lax.broadcasted_iota(jnp.int32, (SP, SLOTS), 0)
     li = lax.broadcasted_iota(jnp.int32, (SP, SLOTS), 1)
     send_hot = []
@@ -386,11 +392,20 @@
     state_faces(0)
     state_faces(1)
     table1 = plane_pack(lambda pt, m, a: uf[pt, m, a], 5, sb1)
-    pl.semaphore_wait(barrier, everyone - 1)
+    pl.semaphore_wait(barrier, len(greeted))
     plane_send(sb1, rb1, 0)
+    if rounds:
+        pass_on(0)
     state_faces(2)
     blocks1 = layer_send(lambda pt, m, a: uf[pt, m, a], 5, zs1, zr1, 1)
 
+    source = [column(fs_ref[f : f + 1, :].astype(F32)) for f in range(4)]
+
+    def hot(keys):
+        rows = [jnp.where(source[2 * a + side] == keys, 1.0, 0.0) for side in range(2) for a in range(2)]
+        return jnp.concatenate(rows, axis=0).astype(BF16)
+
+    hot_own, hot_recv = hot(own_keys), hot(recv_keys)
     for a in range(3):
         wide = jnp.zeros((C, VW), F32)
         face = jnp.zeros((C, FW), F32)
@@ -428,18 +443,34 @@
         if a == 1:
             own = uf[pt, m, a]
             value = jnp.where(wall, own if m % 4 == 0 else -own, value)
-        of[pt, m, a] = jnp.where(fnode < 25, value, uf[pt, m, a])
+        of[pt, m, a] = value
+
+    def face_fields(table, a, rows):
+        primal = [table[0, m, a, rows, :] for m in range(5)]
+        tangent = [table[1, m, a, rows, :] for m in range(5)]
+        return jax.jvp(gradient_fields, (primal,), (tangent,))
+
+    def insides(a):
+        def body(rows):
+            both = face_fields(uf, a, rows)
+            for pt in range(2):
+                for m in range(4):
+                    jf[a, pt, m, rows, :] = both[pt][m]
+
+        blocks_of(body)
 
     def jumps(a):
         def body(rows):
-            primal = ([uf[0, m, a, rows, :] for m in range(5)], [of[0, m, a, rows, :] for m in range(5)])
-            tangent = ([uf[1, m, a, rows, :] for m in range(5)], [of[1, m, a, rows, :] for m in range(5)])
-            jp, jt = jax.jvp(jump_fields, primal, tangent)
-            for m in range(4):
-                jf[a, 0, m, rows, :] = (0.5 * LIFT) * sign * jp[m]
-                jf[a, 1, m, rows, :] = (0.5 * LIFT) * sign * jt[m]
+            both = face_fields(of, a, rows)
+            for pt in range(2):
+                for m in range(4):
+                    jump = both[pt][m] - jf[a, pt, m, rows, :]
+                    jf[a, pt, m, rows, :] = (0.5 * LIFT) * sign * jump
 
         blocks_of(body)
+
+    for a in range(3):
+        insides(a)
 
     def edge_jumps(a, b):
         there, lane = edges[a, b]
@@ -449,12 +480,16 @@
                     qf[a, pt, n] += jnp.where(there, pull(jf[b, pt, f], lane), 0.0)
 
     arrived(zs1, zr1, 1)
+    if rounds:
+        pass_on(1)
     layer_outside(blocks1, zr1, 5, put1)
     jumps(2)
     edge_jumps(0, 2)
     edge_jumps(1, 2)
     arrived(sb1, rb1, 0)
-    plane_outside(own1, rb1, 5, put1)
+    if rounds:
+        pass_on(2)
+    plane_outside(own1, rb1, 5, put1, 3)
     jumps(0)
     jumps(1)
     edge_jumps(0, 1)
@@ -510,6 +545,8 @@
                     g[a, pt, m + 1, rows, :] = scale[a] * (euler[pt][m + 1] - visc[pt][a][m])
 
     blocks_of(fluxes)
+    if rounds:
+        pass_on(3)
     for a in range(3):
         def surfaces(rows):
             primal = ([uf[0, m, a, rows, :] for m in range(5)], [of[0, m, a, rows, :] for m in range(5)])
@@ -549,7 +586,9 @@
     layer_outside(blocks2, zr2, 4, put2)
 
     arrived(sb2, rb2, 2)
-    plane_outside(own2, rb2, 4, put2)
+    if rounds:
+        pass_on(4)
+    plane_outside(own2, rb2, 4, put2, 2)
     lifted = lift(range(3), [s[a, :, :4].reshape(8 * C, FW) for a in range(3)])
     lifted = lifted.reshape(2, 4, C, VW)
     for pt in range(2):
@@ -579,7 +618,7 @@
     table_ref[...] = sta[...].reshape(everyone, 128)
 
 
-def finish(total_count, res, prod, d, table_ref, res_hbm, basis_hbm, kry_ref, basis, sems):
+def finish(total_count, res, prod, d, table_ref, res_hbm, basis_hbm, kry_hbm, basis, kry, sems):
     first = pltpu.make_async_copy(res, res_hbm, sems.at[0])
     first.start()
     lane = lax.broadcasted_iota(jnp.int32, (1, 128), 1)
@@ -594,12 +633,15 @@
     beta = jnp.sqrt(rr * (1.0 / total_count))
     norm = jnp.sqrt(rs * (1.0 / total_count))
     row = jnp.where(lane == 0, coefficient, jnp.where(lane == 1, beta, norm))
-    kry_ref[...] = row[0, :3]
+    kry[...] = row[0, :3]
+    third = pltpu.make_async_copy(kry, kry_hbm, sems.at[2])
+    third.start()
     c, inv = coefficient, 1.0 / beta
     basis[...] = (prod[...] - c[:, :, None] * d[...]) * inv[:, :, None]
     second = pltpu.make_async_copy(basis, basis_hbm, sems.at[1])
     second.start()
     first.wait()
+    third.wait()
     second.wait()
 
 
@@ -643,7 +685,7 @@
             vmem(2, tiles, 8, FW), vmem(2, tiles, 8, FW), vmem(2, C, 2 * FW), vmem(2, C, 2 * FW),
             vmem(1, 128), vmem(ns * np_, 1, 128),
             vmem(2, C, L, width), *[pltpu.VMEM(x.shape, x.dtype) for x in operands[2:]],
-            dma(4), dma(4), dma(2), dma(6),
+            dma(4), dma(4), dma(2), dma(6), pltpu.SemaphoreType.REGULAR((4, 2)),
         ],
         compiler_params=pltpu.CompilerParams(
             collective_id=0, has_side_effects=True, vmem_limit_bytes=40 * 1024 * 1024
@@ -659,8 +701,8 @@
             jax.ShapeDtypeStruct((3,), F32),
         ),
         in_specs=[spec] * 4,
-        out_specs=(hbm, hbm, spec),
-        scratch_shapes=[vmem(C, L, width), dma(2)],
+        out_specs=(hbm, hbm, hbm),
+        scratch_shapes=[vmem(C, L, width), vmem(3), dma(3)],
         compiler_params=pltpu.CompilerParams(vmem_limit_bytes=16 * 1024 * 1024),
         name="finish",
     )(parts, product, own, table)

time: 25.2 us -> 25.1 us (level)
    pallas_call x1, Pallas kernels: 1.38 us -> 0.88 us  [local(): pl.pallas_call(functools.partial(finish, float(state.size * ns * np_)), o...]
    pallas_call x1, Pallas kernels: 23.1 us -> 23.4 us  [local(): pl.pallas_call(functools.partial(kernel, ns, np_), out_shape=(*[jax.Shape...]
where the time goes in v3:
time: 25.1 us; the launch traced here: 24.9 us
  Pallas kernels  24.3 us (97%)
  between operations  0.64 us (3%)
    pallas_call x1, Pallas kernels, local(): pl.pallas_call(functools.partial(kernel, ns, np_), out_shape=(*[jax.Shape...  23.4 us
    pallas_call x1, Pallas kernels, local(): pl.pallas_call(functools.partial(finish, float(state.size * ns * np_)), o...  0.88 us

profile of v3, /device:TPU:0, one launch (start us, length us, event | category | flops | bytes accessed | tf_op | source)
XLA Modules:
  0.0 24.9 jit_solution(12578491098955906373)
XLA Ops:
  0.6 23.4 %navier.1 = (f32[40,2,625]{2,1,0:T(2,128)S(1)}, f32[40,2,625]{2,1,0:T(2,128)S(1)}, f32[40,2,625]{2,1,0:T(2,128)S(1)}, f32[32,128]{1,0:T(8,128)S(1)}) custom-call(f32[40,2,625]{2,1,0:T(2,128)} %x_hbm.1, f32[40,2,625]{2,1,0:T(2,128)} %d_hbm.1, f32[3,2,40]{2,1,0:T(2,128)} %bitcast.2, s32[4,40]{1,0:T(4,128)} %bitcast.3, s32[1,2,33]{2,1,0:T(2,128)} %sr_hbm.1, ...), custom_call_target="tpu_custom_call" | custom-call | tf_op jit(solution)/shard_map/navier/pallas_call | solution.py:670
  24.0 0.9 %finish.1 = (f32[40,2,625]{2,1,0:T(2,128)}, f32[40,2,625]{2,1,0:T(2,128)}, f32[3]{0:T(128)}) custom-call(f32[40,2,625]{2,1,0:T(2,128)S(1)} %get-tuple-element.7.res, f32[40,2,625]{2,1,0:T(2,128)S(1)} %get-tuple-element.8.prod, f32[40,2,625]{2,1,0:T(2,128)S(1)} %get-tuple-element.9.d, f32[32,128]{1,0:T(8,128)S(1)} %get-tuple-element.10.table_ref), custom_call_target="tpu_custom_call" | custom-call | tf_op jit(solution)/shard_map/finish/pallas_call | solution.py:696

commit v4 on v3

--- a/solution.py
+++ b/solution.py
@@ -171,22 +171,20 @@
         return lax.rem(ms + a, ns), lax.rem(mp + b, np_)
 
     everyone = ns * np_
-    rounds = 4 if ns == 8 else 0
-    near = [np_, everyone - np_, *range(1, np_)]
-    greeted = near if rounds else list(range(1, everyone))
+    relayed = ns == 8
+    near = [a * np_ for a in (1, 2, ns - 2, ns - 1)]
+    greeted = near + list(range(1, np_)) if relayed else list(range(1, everyone))
     barrier = pltpu.get_barrier_semaphore()
     for k in greeted:
         pl.semaphore_signal(barrier, inc=1, device_id=peer(k), device_id_type=MESH)
 
-    def pass_on(i):
-        for side, to in ((0, lower), (1, upper)):
-            if i > 0:
-                pl.semaphore_wait(word.at[i - 1, side], 1)
-        if i < rounds:
-            for side, to in ((0, lower), (1, upper)):
-                pl.semaphore_signal(
-                    word.at[i, 1 - side], inc=1, device_id=(to, mp), device_id_type=MESH
-                )
+    def vouch(which, base):
+        for i, k in enumerate(which):
+            pl.semaphore_signal(word.at[base + i], inc=1, device_id=peer(k), device_id_type=MESH)
+
+    def vouched(which, base):
+        for i in range(len(which)):
+            pl.semaphore_wait(word.at[base + i], 1)
 
     fl = lax.broadcasted_iota(jnp.int32, (1, FW), 1)
     vl = lax.broadcasted_iota(jnp.int32, (1, VW), 1)
@@ -302,7 +300,11 @@
         return table
 
     def plane_send(sb, rb, base):
-        remote([(sb.at[0], rb.at[1], (lower, mp)), (sb.at[1], rb.at[0], (upper, mp))], base)
+        far = lax.rem(ms, 2)
+        to = [lax.rem(ms + ns - 1 + 2 * side, ns) for side in (far, 1 - far)]
+        remote(
+            [(sb.at[side], rb.at[1 - side], (t, mp)) for side, t in zip((far, 1 - far), to)], base
+        )
 
     def layer_send(faces, members, zs, zr, base):
         blocks = [swap(faces(0, m, 2), faces(1, m, 2)) for m in range(members)]
@@ -394,8 +396,8 @@
     table1 = plane_pack(lambda pt, m, a: uf[pt, m, a], 5, sb1)
     pl.semaphore_wait(barrier, len(greeted))
     plane_send(sb1, rb1, 0)
-    if rounds:
-        pass_on(0)
+    if relayed:
+        vouch(near, 0)
     state_faces(2)
     blocks1 = layer_send(lambda pt, m, a: uf[pt, m, a], 5, zs1, zr1, 1)
 
@@ -480,15 +482,11 @@
                     qf[a, pt, n] += jnp.where(there, pull(jf[b, pt, f], lane), 0.0)
 
     arrived(zs1, zr1, 1)
-    if rounds:
-        pass_on(1)
     layer_outside(blocks1, zr1, 5, put1)
     jumps(2)
     edge_jumps(0, 2)
     edge_jumps(1, 2)
     arrived(sb1, rb1, 0)
-    if rounds:
-        pass_on(2)
     plane_outside(own1, rb1, 5, put1, 3)
     jumps(0)
     jumps(1)
@@ -545,8 +543,9 @@
                     g[a, pt, m + 1, rows, :] = scale[a] * (euler[pt][m + 1] - visc[pt][a][m])
 
     blocks_of(fluxes)
-    if rounds:
-        pass_on(3)
+    if relayed:
+        vouched(near, 0)
+        vouch(near[1:3], 4)
     for a in range(3):
         def surfaces(rows):
             primal = ([uf[0, m, a, rows, :] for m in range(5)], [of[0, m, a, rows, :] for m in range(5)])
@@ -586,8 +585,8 @@
     layer_outside(blocks2, zr2, 4, put2)
 
     arrived(sb2, rb2, 2)
-    if rounds:
-        pass_on(4)
+    if relayed:
+        vouched(near[1:3], 4)
     plane_outside(own2, rb2, 4, put2, 2)
     lifted = lift(range(3), [s[a, :, :4].reshape(8 * C, FW) for a in range(3)])
     lifted = lifted.reshape(2, 4, C, VW)
@@ -685,7 +684,7 @@
             vmem(2, tiles, 8, FW), vmem(2, tiles, 8, FW), vmem(2, C, 2 * FW), vmem(2, C, 2 * FW),
             vmem(1, 128), vmem(ns * np_, 1, 128),
             vmem(2, C, L, width), *[pltpu.VMEM(x.shape, x.dtype) for x in operands[2:]],
-            dma(4), dma(4), dma(2), dma(6), pltpu.SemaphoreType.REGULAR((4, 2)),
+            dma(4), dma(4), dma(2), dma(6), pltpu.SemaphoreType.REGULAR((6,)),
         ],
         compiler_params=pltpu.CompilerParams(
             collective_id=0, has_side_effects=True, vmem_limit_bytes=40 * 1024 * 1024

time: 25.1 us -> 24.5 us (0.976)
  Pallas kernels: 24.3 us -> 23.7 us
    pallas_call x1, Pallas kernels: 23.4 us -> 22.8 us  [local(): pl.pallas_call(functools.partial(kernel, ns, np_), out_shape=(*[jax.Shape...]
where the time goes in v4:
time: 24.5 us; the launch traced here: 24.3 us
  Pallas kernels  23.7 us (97%)
  between operations  0.64 us (3%)
    pallas_call x1, Pallas kernels, local(): pl.pallas_call(functools.partial(kernel, ns, np_), out_shape=(*[jax.Shape...  22.8 us
    pallas_call x1, Pallas kernels, local(): pl.pallas_call(functools.partial(finish, float(state.size * ns * np_)), o...  0.88 us

profile of v4, /device:TPU:0, one launch (start us, length us, event | category | flops | bytes accessed | tf_op | source)
XLA Modules:
  0.0 24.3 jit_solution(10485650550362640688)
XLA Ops:
  0.6 22.8 %navier.1 = (f32[40,2,625]{2,1,0:T(2,128)S(1)}, f32[40,2,625]{2,1,0:T(2,128)S(1)}, f32[40,2,625]{2,1,0:T(2,128)S(1)}, f32[32,128]{1,0:T(8,128)S(1)}) custom-call(f32[40,2,625]{2,1,0:T(2,128)} %x_hbm.1, f32[40,2,625]{2,1,0:T(2,128)} %d_hbm.1, f32[3,2,40]{2,1,0:T(2,128)} %bitcast.2, s32[4,40]{1,0:T(4,128)} %bitcast.3, s32[1,2,33]{2,1,0:T(2,128)} %sr_hbm.1, ...), custom_call_target="tpu_custom_call" | custom-call | tf_op jit(solution)/shard_map/navier/pallas_call | solution.py:669
  23.5 0.9 %finish.1 = (f32[40,2,625]{2,1,0:T(2,128)}, f32[40,2,625]{2,1,0:T(2,128)}, f32[3]{0:T(128)}) custom-call(f32[40,2,625]{2,1,0:T(2,128)S(1)} %get-tuple-element.7.res, f32[40,2,625]{2,1,0:T(2,128)S(1)} %get-tuple-element.8.prod, f32[40,2,625]{2,1,0:T(2,128)S(1)} %get-tuple-element.9.d, f32[32,128]{1,0:T(8,128)S(1)} %get-tuple-element.10.table_ref), custom_call_target="tpu_custom_call" | custom-call | tf_op jit(solution)/shard_map/finish/pallas_call | solution.py:695

commit v5 on v4

--- a/solution.py
+++ b/solution.py
@@ -141,7 +141,7 @@
     ns, np_,
     x_hbm, d_hbm, metric_hbm, fs_hbm, sr_hbm, key_hbm, ops_hbm,
     res_ref, prod_ref, own_ref, table_ref,
-    u, uf, of, w, jf, q, qf, vf, g, s, r, mv, mf,
+    u, uf, of, w, jf, q, qf, vf, ov, g, s, r, mv, mf, mj,
     sb1, rb1, zs1, zr1, sb2, rb2, zs2, zr2, st, sta,
     xd, metric_ref, fs_ref, sr_ref, key_ref, ops_ref,
     xsend, xrecv, stsem, loads, word,
@@ -178,13 +178,12 @@
     for k in greeted:
         pl.semaphore_signal(barrier, inc=1, device_id=peer(k), device_id_type=MESH)
 
-    def vouch(which, base):
-        for i, k in enumerate(which):
-            pl.semaphore_signal(word.at[base + i], inc=1, device_id=peer(k), device_id_type=MESH)
-
-    def vouched(which, base):
-        for i in range(len(which)):
-            pl.semaphore_wait(word.at[base + i], 1)
+    def vouch(which, i):
+        for k in which:
+            pl.semaphore_signal(word.at[i], inc=1, device_id=peer(k), device_id_type=MESH)
+
+    def vouched(which, i):
+        pl.semaphore_wait(word.at[i], len(which))
 
     fl = lax.broadcasted_iota(jnp.int32, (1, FW), 1)
     vl = lax.broadcasted_iota(jnp.int32, (1, VW), 1)
@@ -275,35 +274,39 @@
         landed(source, xsend.at[base])
 
     def plane_pack(faces, members, sb):
-        blocks = [[swap(faces(0, m, a), faces(1, m, a)) for m in range(members)] for a in range(2)]
+        blocks = [[swap(faces(0, m, a), faces(1, m, a)) for m in members] for a in range(2)]
         table = jnp.concatenate(
             [
-                jnp.concatenate([blocks[a][m][side] for m in range(members)], axis=1)
+                jnp.concatenate([blocks[a][m][side] for m in range(len(members))], axis=1)
                 for side in range(2)
                 for a in range(2)
             ],
             axis=0,
         )
         sent = choose(send_hot, table)
-        for m in range(4):
-            value = sent[:, FW * m : FW * (m + 1)]
-            if members > 4:
+        for i, m in enumerate(members[:4]):
+            value = sent[:, FW * i : FW * (i + 1)]
+            if len(members) > 4:
                 spare = roll(sent[:, 4 * FW :], 25 - 7 * m)
                 value = jnp.where(fnode < 25, value, spare)
             for side in range(2):
                 for b in range(MAIN):
                     at = side * SP + 8 * b
-                    sb[side, 4 * b + m] = value[at : at + 8]
+                    sb[side, MAIN * m + b] = value[at : at + 8]
                 for e in range(REM):
                     at, to = side * SP + 8 * MAIN + e, REM * m + e
                     sb[side, 4 * MAIN + to // 8, to % 8 : to % 8 + 1, :] = value[at : at + 1]
         return table
 
-    def plane_send(sb, rb, base):
+    def plane_send(sb, rb, base, part=slice(None)):
         far = lax.rem(ms, 2)
         to = [lax.rem(ms + ns - 1 + 2 * side, ns) for side in (far, 1 - far)]
         remote(
-            [(sb.at[side], rb.at[1 - side], (t, mp)) for side, t in zip((far, 1 - far), to)], base
+            [
+                (sb.at[side, part], rb.at[1 - side, part], (t, mp))
+                for side, t in zip((far, 1 - far), to)
+            ],
+            base,
         )
 
     def layer_send(faces, members, zs, zr, base):
@@ -325,7 +328,7 @@
         rows = []
         for side in range(2):
             rows += [
-                jnp.concatenate([rb[side, 4 * b + m] for m in range(4)], axis=1)
+                jnp.concatenate([rb[side, MAIN * m + b] for m in range(4)], axis=1)
                 for b in range(MAIN)
             ]
             if REM:
@@ -347,7 +350,10 @@
             received = jnp.concatenate([received, spare], axis=1)
             pad = jnp.where(lax.rem(member, 4) == 0, 1.0, 0.0)
             received = jnp.where(node < 25, received, pad)
-        got = own + choose(hot_recv, received, depth)
+        got = choose(hot_recv, received, depth)
+        spread(got if own is None else own + got, members, put)
+
+    def spread(got, members, put):
         for a in range(2):
             for m in range(members):
                 lanes = slice(FW * m, FW * (m + 1))
@@ -393,7 +399,7 @@
 
     state_faces(0)
     state_faces(1)
-    table1 = plane_pack(lambda pt, m, a: uf[pt, m, a], 5, sb1)
+    table1 = plane_pack(lambda pt, m, a: uf[pt, m, a], range(5), sb1)
     pl.semaphore_wait(barrier, len(greeted))
     plane_send(sb1, rb1, 0)
     if relayed:
@@ -417,6 +423,7 @@
             face = jnp.where(flayer == l, value, face)
         mv[a] = wide
         mf[a] = face
+        mj[a] = (-0.5 * LIFT) * sign * face
 
     def gradients(rows):
         primal = [u[0, m, rows, :] for m in range(5)]
@@ -516,14 +523,21 @@
 
     face_viscous(0)
     face_viscous(1)
-    table2 = plane_pack(lambda pt, m, a: vf[a, pt, m], 4, sb2)
-    plane_send(sb2, rb2, 2)
+    table2 = []
+    for some in (range(0, 2), range(2, 4)):
+        table2.append(plane_pack(lambda pt, m, a: vf[a, pt, m], some, sb2))
+        ends = [MAIN * some[0], MAIN * (some[-1] + 1) if some[-1] < 3 else sb2.shape[1]]
+        plane_send(sb2, rb2, 2, pl.ds(ends[0], ends[1] - ends[0]))
     edge_jumps(2, 0)
     edge_jumps(2, 1)
     face_viscous(2)
     blocks2 = layer_send(lambda pt, m, a: vf[a, pt, m], 4, zs2, zr2, 3)
 
-    own2 = choose(hot_own, table2)
+
+    def put_own(pt, m, a, value):
+        ov[a, pt, m] = jnp.where(wall, vf[a, pt, m], value) if a == 1 else value
+
+    spread(choose(hot_own, jnp.concatenate(table2, axis=1)), 4, put_own)
     for a in range(3):
         q[a] += lift([a], [jf[a].reshape(8 * C, FW)]).reshape(2, 4, C, VW)
 
@@ -545,7 +559,7 @@
     blocks_of(fluxes)
     if relayed:
         vouched(near, 0)
-        vouch(near[1:3], 4)
+        vouch(near[1:3], 1)
     for a in range(3):
         def surfaces(rows):
             primal = ([uf[0, m, a, rows, :] for m in range(5)], [of[0, m, a, rows, :] for m in range(5)])
@@ -557,8 +571,10 @@
             for pt in range(2):
                 s[a, pt, 0, rows, :] = scale * both[pt][0]
                 for m in range(4):
-                    mine = (0.5 * LIFT) * sign * vf[a, pt, m, rows, :]
-                    s[a, pt, m + 1, rows, :] = scale * (both[pt][m + 1] + mine)
+                    inner = vf[a, pt, m, rows, :]
+                    if a < 2:
+                        inner = inner - ov[a, pt, m, rows, :]
+                    s[a, pt, m + 1, rows, :] = scale * both[pt][m + 1] - mj[a, rows, :] * inner
 
         blocks_of(surfaces)
 
@@ -577,17 +593,15 @@
     mine = ratio(pd, dd)
 
     def put2(pt, m, a, value):
-        if a == 1:
-            value = jnp.where(wall, vf[a, pt, m], value)
-        s[a, pt, m] = (-0.5 * LIFT) * sign * mf[a] * value
+        s[a, pt, m] = mj[a] * value
 
     arrived(zs2, zr2, 3)
     layer_outside(blocks2, zr2, 4, put2)
 
     arrived(sb2, rb2, 2)
     if relayed:
-        vouched(near[1:3], 4)
-    plane_outside(own2, rb2, 4, put2, 2)
+        vouched(near[1:3], 1)
+    plane_outside(None, rb2, 4, put2, 2)
     lifted = lift(range(3), [s[a, :, :4].reshape(8 * C, FW) for a in range(3)])
     lifted = lifted.reshape(2, 4, C, VW)
     for pt in range(2):
@@ -677,14 +691,14 @@
         scratch_shapes=[
             vmem(2, 5, C, VW), vmem(2, 5, 3, C, FW), vmem(2, 5, 3, C, FW),
             vmem(2, 4, C, VW), vmem(3, 2, 4, C, FW), vmem(3, 2, 4, C, VW),
-            vmem(3, 2, 8, C, FW), vmem(3, 2, 4, C, FW),
+            vmem(3, 2, 8, C, FW), vmem(3, 2, 4, C, FW), vmem(2, 2, 4, C, FW),
             vmem(3, 2, 5, C, VW), vmem(3, 2, 5, C, FW), vmem(2, 5, C, VW),
-            vmem(3, C, VW), vmem(3, C, FW),
+            vmem(3, C, VW), vmem(3, C, FW), vmem(3, C, FW),
             vmem(2, tiles, 8, FW), vmem(2, tiles, 8, FW), vmem(2, C, 3 * FW), vmem(2, C, 3 * FW),
             vmem(2, tiles, 8, FW), vmem(2, tiles, 8, FW), vmem(2, C, 2 * FW), vmem(2, C, 2 * FW),
             vmem(1, 128), vmem(ns * np_, 1, 128),
             vmem(2, C, L, width), *[pltpu.VMEM(x.shape, x.dtype) for x in operands[2:]],
-            dma(4), dma(4), dma(2), dma(6), pltpu.SemaphoreType.REGULAR((6,)),
+            dma(4), dma(4), dma(2), dma(6), pltpu.SemaphoreType.REGULAR((2,)),
         ],
         compiler_params=pltpu.CompilerParams(
             collective_id=0, has_side_effects=True, vmem_limit_bytes=40 * 1024 * 1024

time: 24.5 us -> 24.3 us (level)
  no operation moved by 1% of the time
where the time goes in v5:
time: 24.3 us; the launch traced here: 24.1 us
  Pallas kernels  23.5 us (97%)
  between operations  0.64 us (3%)
    pallas_call x1, Pallas kernels, local(): pl.pallas_call(functools.partial(kernel, ns, np_), out_shape=(*[jax.Shape...  22.6 us
    pallas_call x1, Pallas kernels, local(): pl.pallas_call(functools.partial(finish, float(state.size * ns * np_)), o...  0.88 us

profile of v5, /device:TPU:0, one launch (start us, length us, event | category | flops | bytes accessed | tf_op | source)
XLA Modules:
  0.0 24.1 jit_solution(14378203119127531782)
XLA Ops:
  0.6 22.6 %navier.1 = (f32[40,2,625]{2,1,0:T(2,128)S(1)}, f32[40,2,625]{2,1,0:T(2,128)S(1)}, f32[40,2,625]{2,1,0:T(2,128)S(1)}, f32[32,128]{1,0:T(8,128)S(1)}) custom-call(f32[40,2,625]{2,1,0:T(2,128)} %x_hbm.1, f32[40,2,625]{2,1,0:T(2,128)} %d_hbm.1, f32[3,2,40]{2,1,0:T(2,128)} %bitcast.2, s32[4,40]{1,0:T(4,128)} %bitcast.3, s32[1,2,33]{2,1,0:T(2,128)} %sr_hbm.1, ...), custom_call_target="tpu_custom_call" | custom-call | tf_op jit(solution)/shard_map/navier/pallas_call | solution.py:683
  23.2 0.9 %finish.1 = (f32[40,2,625]{2,1,0:T(2,128)}, f32[40,2,625]{2,1,0:T(2,128)}, f32[3]{0:T(128)}) custom-call(f32[40,2,625]{2,1,0:T(2,128)S(1)} %get-tuple-element.7.res, f32[40,2,625]{2,1,0:T(2,128)S(1)} %get-tuple-element.8.prod, f32[40,2,625]{2,1,0:T(2,128)S(1)} %get-tuple-element.9.d, f32[32,128]{1,0:T(8,128)S(1)} %get-tuple-element.10.table_ref), custom_call_target="tpu_custom_call" | custom-call | tf_op jit(solution)/shard_map/finish/pallas_call | solution.py:709
